TPU v7x, 8 devices: a whole 2x2x1 slice. The times are simulated.
8 devices in a mesh: dp: 2 (over z, y), ep: 4 (over x, core).
Axes of the slice: x: 2, y: 2, z: 1, core: 2. Of those that a mesh axis runs over, the one named last changes fastest.
Arguments:
- x_norm: bfloat16 [2048, 1536], P(('dp', 'ep'))
- route_idx: int32 [2048, 8], P(('dp', 'ep'))
- w_router: bfloat16 [1536, 40], replicated
- w_gate: bfloat16 [40, 1536, 512], P('ep')
- w_up: bfloat16 [40, 1536, 512], P('ep')
- w_down: bfloat16 [40, 512, 1536], P('ep')
- grad_out: bfloat16 [2048, 1536], P(('dp', 'ep'))
Outputs:
- output 1: bfloat16 [2048, 1536], P(('dp', 'ep'))
- output 2: float32 [40, 1536, 512], P('ep')
- output 3: float32 [40, 1536, 512], P('ep')
- output 4: float32 [40, 512, 1536], P('ep')
- output 5: float32 [1536, 40], replicated
All inputs are finite; a program needn't handle non-finite values.
Results may differ from a plain program's by a relative error of at most 0.00564174.
Values are sent between devices in bfloat16 or wider.
A program may use at most 1 GiB of HBM per device.

v0:
```python
import functools

import jax
import jax.numpy as jnp
from jax import lax
from jax.experimental import pallas as pl
from jax.experimental.pallas import tpu as pltpu
from jax.sharding import PartitionSpec as P

SLOTS = 64
EXTRA = 96
PAD = 16
F32 = jnp.float32
BF16 = jnp.bfloat16
VMEM_LIMIT = 67043328
MESH = pl.DeviceIdType.MESH


def nt_dot(a, b):
    return lax.dot_general(a, b, (((1,), (1,)), ((), ())), preferred_element_type=F32)


def tn_dot(a, b):
    return lax.dot_general(a, b, (((0,), (0,)), ((), ())), preferred_element_type=F32)


def nn_dot(a, b):
    return jnp.dot(a, b, preferred_element_type=F32)


def slot_mask(rank_row, rows, first):
    slot = lax.broadcasted_iota(jnp.int32, (rows, rank_row.shape[1]), 0) + first
    return slot.astype(F32) == rank_row


def hot_rows(rank):
    return jnp.max(rank, axis=1, keepdims=True) >= SLOTS


def extra_rank(rank):
    return jnp.max(jnp.where(hot_rows(rank), rank, -1.0), axis=0, keepdims=True)


def route_kernel(groups, per_group, x_ref, wr_ref, idx_ref, out_ref):
    rows, toks = groups * PAD, x_ref.shape[0]
    logits = nt_dot(wr_ref[...], x_ref[...])
    row = lax.broadcasted_iota(jnp.int32, (rows, toks), 0)
    expert = jnp.where(row % PAD < per_group, (row // PAD) * per_group + row % PAD, -1)
    chosen = expert == idx_ref[0:1, :]
    for k in range(1, idx_ref.shape[0]):
        chosen = chosen | (expert == idx_ref[k : k + 1, :])
    before = lax.broadcasted_iota(jnp.int32, (toks, toks), 0) < lax.broadcasted_iota(jnp.int32, (toks, toks), 1)
    rank = nn_dot(chosen.astype(F32).astype(BF16), before.astype(F32).astype(BF16))
    top = jnp.max(jnp.where(chosen, logits, -jnp.inf), axis=0, keepdims=True)
    weight = jnp.where(chosen, jnp.exp(logits - top), 0.0)
    prob = weight / jnp.sum(weight, axis=0, keepdims=True)
    out_ref[0] = jnp.where(chosen, rank, -1.0).reshape(groups, PAD, toks)
    out_ref[1] = prob.reshape(groups, PAD, toks)


def gather_rows(me, per_group, m_ref, x_ref, g_ref, x_out, d_out, g_out):
    step = per_group // 2

    def emit(masks, probs, where):
        pick = jnp.concatenate([m.astype(F32).astype(BF16) for m in masks], axis=0)
        gate = jnp.concatenate([jnp.sum(jnp.where(m, p, 0.0), axis=1, keepdims=True) for m, p in zip(masks, probs)], axis=0)
        x_out[where, :] = nn_dot(pick, x_ref[...]).astype(BF16)
        rows_g = nn_dot(pick, g_ref[...])
        if g_out is not None:
            g_out[where, :] = rows_g.astype(BF16)
        d_out[where, :] = (gate * rows_g).astype(BF16)

    def part(i, carry):
        ranks = [m_ref[0, me, pl.ds(i * step + k, 1), :] for k in range(step)]
        probs = [m_ref[1, me, pl.ds(i * step + k, 1), :] for k in range(step)]
        emit([slot_mask(r, SLOTS, 0) for r in ranks], probs, pl.ds(pl.multiple_of(i * (step * SLOTS), SLOTS), step * SLOTS))
        return carry

    lax.fori_loop(0, 2, part, 0)
    rank, prob = m_ref[0, me], m_ref[1, me]
    prob_hot = jnp.sum(jnp.where(hot_rows(rank), prob, 0.0), axis=0, keepdims=True)
    emit([slot_mask(extra_rank(rank), EXTRA, SLOTS)], [prob_hot], pl.ds(per_group * SLOTS, EXTRA))


class Stage:
    def __init__(self, main, bufs, sems, outs):
        self.main, self.bufs, self.sems, self.outs, self.busy = main, bufs, sems, outs, {}

    def gather(self, i, kinds, me, per_group, m_ref, x_ref, g_ref):
        slot = i % 2
        self.drain(slot)
        views = [self.bufs[k].at[slot] for k in range(kinds)]
        gather_rows(me, per_group, m_ref, x_ref, g_ref, *(views + [None])[:3])
        copies = []
        for k in range(kinds):
            copies.append(pltpu.make_async_copy(views[k].at[pl.ds(0, self.main)], self.outs[2 * k].at[i], self.sems.at[slot, 2 * k]))
            copies.append(pltpu.make_async_copy(views[k].at[pl.ds(self.main, EXTRA)], self.outs[2 * k + 1].at[i], self.sems.at[slot, 2 * k + 1]))
        for c in copies:
            c.start()
        self.busy[slot] = copies

    def drain(self, slot):
        for c in self.busy.pop(slot, ()):
            c.wait()


def device_of(bit):
    return (lax.axis_index("dp") ^ (bit >> 2), lax.axis_index("ep") ^ (bit & 3))


def greet(bits):
    barrier = pltpu.get_barrier_semaphore()
    for bit in bits:
        pl.semaphore_signal(barrier, inc=1, device_id=device_of(bit), device_id_type=MESH)
    pl.semaphore_wait(barrier, len(bits))


def near_kernel(per_group, x_ref, g_ref, m_ref, *refs):
    rows_out, (xs_out, ms_out, g2_out) = refs[:6], refs[6:9]
    x_in, g_in, m_in, st_x, st_d, st_g, send, recv, out_sem, st_sem = refs[9:]
    me = lax.axis_index("ep")
    greet((1, 2, 4))
    own = (x_ref, g_ref, m_ref)
    land = lambda s: (x_in.at[s - 1], g_in.at[s - 1], m_in.at[s - 1])

    def push(srcs, s, bit):
        copies = []
        for k, (src, dst) in enumerate(zip(srcs, land(s))):
            copies.append(pltpu.make_async_remote_copy(src_ref=src, dst_ref=dst, send_sem=send.at[s - 1, k], recv_sem=recv.at[s - 1, k], device_id=device_of(bit), device_id_type=MESH))
        for c in copies:
            c.start()
        return copies

    flights = {2: push(own, 2, 2), 4: push(own, 4, 4), 1: push(own, 1, 1)}
    outs = []

    def arrive(s):
        for c in flights[s]:
            c.wait_recv()
        keep = [pltpu.make_async_copy(x_in.at[s - 1], xs_out.at[s - 1], out_sem.at[s - 1, 0]), pltpu.make_async_copy(m_in.at[s - 1], ms_out.at[s - 1], out_sem.at[s - 1, 1])]
        if s == 2:
            keep.append(pltpu.make_async_copy(g_in.at[s - 1], g2_out, out_sem.at[s - 1, 2]))
        for c in keep:
            c.start()
        outs.extend(keep)

    stage = Stage(per_group * SLOTS, (st_x, st_d, st_g), st_sem, rows_out)

    def gather(s):
        x, g, m = own if s == 0 else land(s)
        stage.gather(s, 3 if s < 4 else 2, me, per_group, m, x, g)

    gather(0)
    arrive(1)
    gather(1)
    arrive(2)
    flights[3] = push(land(2), 3, 1)
    arrive(4)
    flights[5] = push(land(4), 5, 1)
    gather(2)
    arrive(3)
    gather(3)
    gather(4)
    arrive(5)
    gather(5)
    stage.drain(0)
    stage.drain(1)
    for s in flights:
        for c in flights[s]:
            c.wait_send()
    for c in outs:
        c.wait()


def back_kernel(per_group, x6_ref, g6_ref, m6_ref, q_ref, gx_ref, *refs):
    rows_out, (x7_ref, m7_ref, me_ref, peer_ref, q_out) = refs[:4], refs[4:9]
    x7_in, g7_in, m7_in, part_in, q_in, st_x, st_d, send, recv, q_send, q_recv, ld_sem, st_sem = refs[9:]
    me = lax.axis_index("ep")
    n_dev = q_in.shape[0]
    greet(tuple(range(1, n_dev)))

    def push(src, dst, i, bit, s_sem, r_sem):
        c = pltpu.make_async_remote_copy(src_ref=src, dst_ref=dst, send_sem=s_sem.at[i], recv_sem=r_sem.at[i], device_id=device_of(bit), device_id_type=MESH)
        c.start()
        return c

    qs = [push(q_ref, q_in.at[bit], bit, bit, q_send, q_recv) for bit in range(1, n_dev)]
    sevens = [push(src, dst, i, 1, send, recv) for i, (src, dst) in enumerate(((x6_ref, x7_in), (g6_ref, g7_in), (m6_ref, m7_in)))]
    parts = [push(gx_ref.at[2 * h + 1], part_in.at[h], 3 + h, 1, send, recv) for h in range(2)]
    loads = [pltpu.make_async_copy(gx_ref.at[2 * h], dst, ld_sem.at[h]) for h, dst in enumerate((me_ref, peer_ref))]
    for c in loads:
        c.start()
    stage = Stage(per_group * SLOTS, (st_x, st_d), st_sem, rows_out)
    stage.gather(0, 2, me, per_group, m6_ref, x6_ref, g6_ref)
    for c in sevens:
        c.wait_recv()
    stage.gather(1, 2, me, per_group, m7_in, x7_in, g7_in)
    x7_ref[...] = x7_in[...]
    m7_ref[...] = m7_in[...]
    q_out[0] = q_ref[...]
    for bit, c in enumerate(qs):
        c.wait_recv()
        q_out[bit + 1] = q_in[bit + 1]
    for h, dst in enumerate((me_ref, peer_ref)):
        loads[h].wait()
        parts[h].wait_recv()
        dst[...] += part_in[h]
    stage.drain(0)
    stage.drain(1)
    for c in qs + sevens + parts:
        c.wait_send()


def expert_math(x, d, w1, w3, w2):
    z1 = nn_dot(x, w1)
    z3 = nn_dot(x, w3)
    sig = jax.nn.sigmoid(z1)
    silu = z1 * sig
    act = (silu * z3).astype(BF16)
    d_act = nt_dot(d, w2)
    dz1 = (d_act * z3 * sig * (1.0 + z1 * (1.0 - sig))).astype(BF16)
    dz3 = (d_act * silu).astype(BF16)
    return act, dz1, dz3


def flat(ref, first=0, count=None):
    v = ref[first : first + (count or ref.shape[0])]
    return v.reshape(v.shape[0] * v.shape[1], v.shape[2])


def pass1_kernel(n_sh, per_group, hot_ref, ep_ref, w1_ref, w3_ref, w2_ref, x_ref, d_ref, g_ref, xo_ref, do_ref, go_ref, *refs):
    m_refs = refs[:n_sh]
    gx_ref, q_ref, act_ref, dz_ref, r_scr = refs[n_sh:]
    e = pl.program_id(0)
    ff = w1_ref.shape[2]
    w1, w3, w2 = w1_ref[0], w3_ref[0], w2_ref[0]
    base = per_group * SLOTS

    def token_math(x, d, g):
        act, dz1, dz3 = expert_math(x, d, w1, w3, w2)
        q = jnp.sum(nn_dot(act, w2) * g.astype(F32), axis=1, keepdims=True)
        r = (nt_dot(dz1, w1) + nt_dot(dz3, w3)).astype(BF16)
        return act, dz1, dz3, q, r

    @pl.when(e == 0)
    def _():
        r_scr[:, base : base + EXTRA, :] = jnp.zeros((n_sh, EXTRA, r_scr.shape[2]), BF16)
        q_ref[...] = jnp.zeros_like(q_ref)

    act, dz1, dz3, q, r = token_math(flat(x_ref), flat(d_ref), flat(g_ref))
    act_ref[0] = act
    dz_ref[0, :, :ff] = dz1
    dz_ref[0, :, ff:] = dz3
    for j in range(n_sh):
        rank_row = m_refs[j][0, 0, pl.ds(e, 1), :]
        mask = slot_mask(rank_row, SLOTS, 0)
        q_ref[j, pl.ds(e, 1), :] = jnp.sum(jnp.where(mask, q[j * SLOTS : (j + 1) * SLOTS], 0.0), axis=0, keepdims=True)
        r_scr[j, pl.ds(pl.multiple_of(e * SLOTS, SLOTS), SLOTS), :] = r[j * SLOTS : (j + 1) * SLOTS]

    is_hot = [hot_ref[e * n_sh + j] for j in range(n_sh)]

    @pl.when(sum(is_hot) > 0)
    def _():
        d = jnp.concatenate([do_ref[j] * is_hot[j].astype(F32).astype(BF16) for j in range(n_sh)], axis=0)
        _, _, _, q, r = token_math(flat(xo_ref), d, flat(go_ref))
        for j in range(n_sh):

            @pl.when(is_hot[j] > 0)
            def _():
                rank_row = m_refs[j][0, 0, pl.ds(e, 1), :]
                mask = slot_mask(rank_row, EXTRA, SLOTS)
                q_ref[j, pl.ds(e, 1), :] += jnp.sum(jnp.where(mask, q[j * EXTRA : (j + 1) * EXTRA], 0.0), axis=0, keepdims=True)
                r_scr[j, base : base + EXTRA, :] = r[j * EXTRA : (j + 1) * EXTRA]

    @pl.when(e == per_group - 1)
    def _():
        for j in range(n_sh):
            rank = m_refs[j][0, 0]
            masks = [slot_mask(rank[i : i + 1, :], SLOTS, 0) for i in range(per_group)]
            masks.append(slot_mask(extra_rank(rank), EXTRA, SLOTS))
            pick = jnp.concatenate([m.astype(F32).astype(BF16) for m in masks], axis=0)
            gx_ref[j] = tn_dot(pick, r_scr[j])


def pass2_kernel(n_near, hot_ref, w1_ref, w3_ref, w2_ref, act_ref, dz_ref, x_ref, d_ref, xf_ref, df_ref, xo_ref, do_ref, xfo_ref, dfo_ref, g1_ref, g3_ref, g2_ref):
    n_sh = x_ref.shape[0] + xf_ref.shape[0]
    e = pl.program_id(0)
    ff = w1_ref.shape[2]
    w1, w3, w2 = w1_ref[0], w3_ref[0], w2_ref[0]
    n_mid = x_ref.shape[0] - n_near
    x = jnp.concatenate([flat(x_ref), flat(xf_ref)], axis=0)
    d = jnp.concatenate([flat(d_ref), flat(df_ref)], axis=0)
    near = n_near * SLOTS
    act, dz1, dz3 = expert_math(x[near:], d[near:], w1, w3, w2)
    g1_ref[0] = tn_dot(x, jnp.concatenate([dz_ref[0, :, :ff], dz1], axis=0))
    g3_ref[0] = tn_dot(x, jnp.concatenate([dz_ref[0, :, ff:], dz3], axis=0))
    g2_ref[0] = tn_dot(jnp.concatenate([act_ref[0], act], axis=0), d)

    hot = [hot_ref[e * n_sh + j] for j in range(n_sh)]
    for far in range(2):
        is_hot = hot[n_near:] if far else hot[:n_near]

        @pl.when(sum(is_hot) > 0)
        def _():
            if far:
                x = jnp.concatenate([flat(xo_ref, n_near, n_mid), flat(xfo_ref)], axis=0)
                ds = [do_ref[n_near + i] for i in range(n_mid)] + [dfo_ref[i] for i in range(n_near - n_mid)]
            else:
                x = flat(xo_ref, 0, n_near)
                ds = [do_ref[i] for i in range(n_near)]
            d = jnp.concatenate([v * h.astype(F32).astype(BF16) for v, h in zip(ds, is_hot)], axis=0)
            act, dz1, dz3 = expert_math(x, d, w1, w3, w2)
            g1_ref[0] += tn_dot(x, dz1)
            g3_ref[0] += tn_dot(x, dz3)
            g2_ref[0] += tn_dot(act, d)


def finish_kernel(groups, ep_ref, keep_ref, far_ref, wr_ref, x0_ref, xs_ref, x6_ref, x7_ref, m0_ref, ms_ref, m6_ref, m7_ref, q_ref, gx_ref, gr_ref):
    n_sh = q_ref.shape[0]
    x_refs = [x0_ref] + [xs_ref.at[i] for i in range(n_sh - 3)] + [x6_ref, x7_ref]
    m_refs = [m0_ref] + [ms_ref.at[i] for i in range(n_sh - 3)] + [m6_ref, m7_ref]
    ep = ep_ref[0]
    for s in range(n_sh):
        d, j = divmod(s, groups)
        q = jnp.concatenate([q_ref[d * groups + (ep ^ a), (ep ^ a) ^ j] for a in range(groups)], axis=0)
        p = m_refs[s][1].reshape(groups * PAD, q.shape[1])
        dl = p * (q - jnp.sum(p * q, axis=0, keepdims=True))
        dl = dl.astype(BF16)
        term = nn_dot(dl, x_refs[s][...])
        if s == 0:
            du = tn_dot(dl, wr_ref[...])
            gx_ref[...] = (keep_ref[...] + far_ref[...] + du).astype(BF16)
            gr_ref[...] = term
        else:
            gr_ref[...] += term


def solution(mesh):
    dp, ep = mesh.shape["dp"], mesh.shape["ep"]
    n_dev = dp * ep
    tok_spec = P(("dp", "ep"), None)
    exp_spec = P("ep", None, None)

    def swap(v, bit):
        return lax.ppermute(v, ("dp", "ep"), [(s, s ^ bit) for s in range(n_dev)])

    def device_step(x_loc, route_idx, w_router, w_gate, w_up, w_down, dy_loc):
        toks, dim = x_loc.shape
        n_exp = w_router.shape[1]
        n_loc, _, ff = w_gate.shape
        me = lax.axis_index("ep")
        ep_arr = me.reshape(1).astype(jnp.int32)
        vmem = pl.BlockSpec(memory_space=pltpu.VMEM)
        params = pltpu.CompilerParams(vmem_limit_bytes=VMEM_LIMIT)

        wr_rows = jnp.pad(w_router.T.reshape(ep, n_loc, dim), ((0, 0), (0, PAD - n_loc), (0, 0))).reshape(ep * PAD, dim)
        route = pl.pallas_call(
            functools.partial(route_kernel, ep, n_loc),
            out_shape=jax.ShapeDtypeStruct((2, ep, PAD, toks), F32),
            in_specs=[vmem] * 3,
            out_specs=vmem,
            compiler_params=params,
            cost_estimate=pl.CostEstimate(flops=10**9, bytes_accessed=10**6, transcendentals=0),
            name="route",
        )(x_loc, wr_rows, route_idx.T)

        hbm = pl.BlockSpec(memory_space=pl.ANY)
        main = n_loc * SLOTS
        sds = jax.ShapeDtypeStruct
        m_shape = route.shape
        near_out = pl.pallas_call(
            functools.partial(near_kernel, n_loc),
            out_shape=[
                sds((6, main, dim), BF16),
                sds((6, EXTRA, dim), BF16),
                sds((6, main, dim), BF16),
                sds((6, EXTRA, dim), BF16),
                sds((4, main, dim), BF16),
                sds((4, EXTRA, dim), BF16),
                sds((5, toks, dim), BF16),
                sds((5,) + m_shape, F32),
                sds((toks, dim), BF16),
            ],
            in_specs=[vmem] * 3,
            out_specs=[hbm] * 9,
            scratch_shapes=[
                pltpu.VMEM((5, toks, dim), BF16),
                pltpu.VMEM((5, toks, dim), BF16),
                pltpu.VMEM((5,) + m_shape, F32),
                pltpu.VMEM((2, main + EXTRA, dim), BF16),
                pltpu.VMEM((2, main + EXTRA, dim), BF16),
                pltpu.VMEM((2, main + EXTRA, dim), BF16),
                pltpu.SemaphoreType.DMA((5, 3)),
                pltpu.SemaphoreType.DMA((5, 3)),
                pltpu.SemaphoreType.DMA((5, 3)),
                pltpu.SemaphoreType.DMA((2, 6)),
            ],
            compiler_params=pltpu.CompilerParams(collective_id=0, has_side_effects=True, vmem_limit_bytes=VMEM_LIMIT),
            cost_estimate=pl.CostEstimate(flops=2 * 10**10, bytes_accessed=5 * 10**7, transcendentals=0),
            name="near",
        )(x_loc, dy_loc, route)
        x_rows, x_more, d_rows, d_more, g_rows, g_more, xs, ms, g2 = near_out
        x6, g6, m6 = swap(xs[1], 4), swap(g2, 4), swap(ms[1], 4)

        def hot_flags(m_list):
            ranks = jnp.stack([lax.dynamic_index_in_dim(m[0], me, 0, keepdims=False) for m in m_list])
            return (jnp.max(ranks, axis=2) >= SLOTS).astype(jnp.int32)[:, :n_loc].T.reshape(-1)

        m_near = [route] + [ms[i] for i in range(5)]
        w_specs = lambda im: [pl.BlockSpec((1, dim, ff), im), pl.BlockSpec((1, dim, ff), im), pl.BlockSpec((1, ff, dim), im)]

        im3 = lambda e, hot, ep_ref: (e, 0, 0)
        rows_at = lambda e, hot, ep_ref: (0, e, 0)
        fix = lambda shape: pl.BlockSpec(shape, lambda e, hot, ep_ref: (0,) * len(shape), pipeline_mode=pl.Buffered(1))
        n_row = ep * SLOTS
        gx_part, q_loc, act, dz = pl.pallas_call(
            functools.partial(pass1_kernel, ep, n_loc),
            out_shape=[
                jax.ShapeDtypeStruct((ep, toks, dim), F32),
                jax.ShapeDtypeStruct((ep, PAD, toks), F32),
                jax.ShapeDtypeStruct((n_loc, n_row, ff), BF16),
                jax.ShapeDtypeStruct((n_loc, n_row, 2 * ff), BF16),
            ],
            grid_spec=pltpu.PrefetchScalarGridSpec(
                num_scalar_prefetch=2,
                grid=(n_loc,),
                in_specs=w_specs(im3)
                + [pl.BlockSpec((ep, SLOTS, dim), rows_at)] * 3
                + [fix((ep, EXTRA, dim))] * 3
                + [pl.BlockSpec((1, 1, PAD, toks), lambda e, hot, ep_ref: (0, ep_ref[0], 0, 0))] * ep,
                out_specs=[fix((ep, toks, dim)), fix((ep, PAD, toks)), pl.BlockSpec((1, n_row, ff), im3), pl.BlockSpec((1, n_row, 2 * ff), im3)],
                scratch_shapes=[pltpu.VMEM((ep, n_loc * SLOTS + EXTRA, dim), BF16)],
            ),
            compiler_params=params,
            cost_estimate=pl.CostEstimate(flops=4 * 10**10, bytes_accessed=10**8, transcendentals=0),
            name="pass1",
        )(
            hot_flags(m_near[:ep]),
            ep_arr,
            w_gate,
            w_up,
            w_down,
            x_rows,
            d_rows,
            g_rows,
            x_more,
            d_more,
            g_more,
            *m_near[:ep],
        )

        sum_shape = sds((toks, dim), F32)
        back_out = pl.pallas_call(
            functools.partial(back_kernel, n_loc),
            out_shape=[
                sds((2, main, dim), BF16),
                sds((2, EXTRA, dim), BF16),
                sds((2, main, dim), BF16),
                sds((2, EXTRA, dim), BF16),
                sds((toks, dim), BF16),
                sds(m_shape, F32),
                sum_shape,
                sum_shape,
                sds((n_dev, ep, PAD, toks), F32),
            ],
            in_specs=[vmem] * 4 + [hbm],
            out_specs=[hbm] * 4 + [vmem] * 5,
            scratch_shapes=[
                pltpu.VMEM((toks, dim), BF16),
                pltpu.VMEM((toks, dim), BF16),
                pltpu.VMEM(m_shape, F32),
                pltpu.VMEM((2, toks, dim), F32),
                pltpu.VMEM((n_dev, ep, PAD, toks), F32),
                pltpu.VMEM((2, main + EXTRA, dim), BF16),
                pltpu.VMEM((2, main + EXTRA, dim), BF16),
                pltpu.SemaphoreType.DMA((5,)),
                pltpu.SemaphoreType.DMA((5,)),
                pltpu.SemaphoreType.DMA((n_dev,)),
                pltpu.SemaphoreType.DMA((n_dev,)),
                pltpu.SemaphoreType.DMA((2,)),
                pltpu.SemaphoreType.DMA((2, 4)),
            ],
            compiler_params=pltpu.CompilerParams(collective_id=1, has_side_effects=True, vmem_limit_bytes=VMEM_LIMIT),
            cost_estimate=pl.CostEstimate(flops=8 * 10**9, bytes_accessed=5 * 10**7, transcendentals=0),
            name="back",
        )(x6, g6, m6, q_loc, gx_part)
        xf_rows, xf_more, df_rows, df_more, x7, m7, for_me, for_peer, q_all = back_out
        from_peer = swap(for_peer, 2)

        im3 = lambda e, hot: (e, 0, 0)
        rows_at = lambda e, hot: (0, e, 0)
        fix = lambda shape: pl.BlockSpec(shape, lambda e, hot: (0,) * len(shape), pipeline_mode=pl.Buffered(1))
        grad_gate, grad_up, grad_down = pl.pallas_call(
            functools.partial(pass2_kernel, ep),
            out_shape=[
                jax.ShapeDtypeStruct((n_loc, dim, ff), F32),
                jax.ShapeDtypeStruct((n_loc, dim, ff), F32),
                jax.ShapeDtypeStruct((n_loc, ff, dim), F32),
            ],
            grid_spec=pltpu.PrefetchScalarGridSpec(
                num_scalar_prefetch=1,
                grid=(n_loc,),
                in_specs=w_specs(im3)
                + [pl.BlockSpec((1, n_row, ff), im3), pl.BlockSpec((1, n_row, 2 * ff), im3)]
                + [pl.BlockSpec((6, SLOTS, dim), rows_at)] * 2
                + [pl.BlockSpec((2, SLOTS, dim), rows_at)] * 2
                + [fix((6, EXTRA, dim))] * 2
                + [fix((2, EXTRA, dim))] * 2,
                out_specs=w_specs(im3),
            ),
            compiler_params=params,
            cost_estimate=pl.CostEstimate(flops=6 * 10**10, bytes_accessed=2 * 10**8, transcendentals=0),
            name="pass2",
        )(
            hot_flags(m_near + [m6, m7]),
            w_gate,
            w_up,
            w_down,
            act,
            dz,
            x_rows,
            d_rows,
            xf_rows,
            df_rows,
            x_more,
            d_more,
            xf_more,
            df_more,
        )

        fixed = lambda shape: pl.BlockSpec(shape, lambda i, ep_ref: (0,) * len(shape))
        grad_x, grad_rt = pl.pallas_call(
            functools.partial(finish_kernel, ep),
            out_shape=[jax.ShapeDtypeStruct((toks, dim), BF16), jax.ShapeDtypeStruct((ep * PAD, dim), F32)],
            grid_spec=pltpu.PrefetchScalarGridSpec(
                num_scalar_prefetch=1,
                grid=(1,),
                in_specs=[fixed((toks, dim)), fixed((toks, dim)), fixed((ep * PAD, dim))]
                + [fixed(v.shape) for v in (x_loc, xs, x6, x7, route, ms, m6, m7, q_all)],
                out_specs=[fixed((toks, dim)), fixed((ep * PAD, dim))],
            ),
            compiler_params=params,
            cost_estimate=pl.CostEstimate(flops=4 * 10**9, bytes_accessed=10**7, transcendentals=0),
            name="finish",
        )(ep_arr, for_me, from_peer, wr_rows, x_loc, xs, x6, x7, route, ms, m6, m7, q_all)
        grad_router = grad_rt.reshape(ep, PAD, dim)[:, :n_loc].reshape(n_exp, dim).T
        return grad_x, grad_gate, grad_up, grad_down, grad_router

    return jax.shard_map(device_step, mesh=mesh, in_specs=(tok_spec, tok_spec, P(), exp_spec, exp_spec, exp_spec, tok_spec), out_specs=(tok_spec, exp_spec, exp_spec, exp_spec, P()), check_vma=False)
```

profile of v0, /device:TPU:3, one launch (start us, length us, event | category | flops | bytes accessed | tf_op | source)
XLA Modules:
  0.0 227.3 jit_solution(10047901895766273170)
XLA Ops:
  0.6 0.9 reshape.54
  1.6 0.7 pad.4
  2.3 2.3 %route.1.m_ref.refs_0_.m0_ref = f32[2,4,16,256]{3,2,1,0:T(8,128)} custom-call(bf16[256,1536]{1,0:T(8,128)(2,1)} %x0_ref.1, bf16[64,1536]{1,0:T(8,128)(2,1)} %bitcast.41, s32[8,256]{1,0:T(8,128)} %bitcast.44), custom_call_target="tpu_custom_call" | custom-call | flops 1000000000 | bytes 1000000 | tf_op jit(solution)/shard_map/route/pallas_call | solution.py:357
  4.6 53.2 %near.1 = (bf16[6,640,1536]{2,1,0:T(8,128)(2,1)}, bf16[6,96,1536]{2,1,0:T(8,128)(2,1)}, bf16[6,640,1536]{2,1,0:T(8,128)(2,1)}, bf16[6,96,1536]{2,1,0:T(8,128)(2,...) custom-call(bf16[256,1536]{1,0:T(8,128)(2,1)} %x0_ref.1, ...), custom_call_target="tpu_custom_call" | custom-call | flops 20000000000 | bytes 50000000 | tf_op jit(solution)/shard_map/near/pallas_call | solution.py:371
  57.8 1.8 slice_bitcast_fusion.1
  59.6 1.2 collective-permute-start.2
  60.8 2.1 slice_bitcast_fusion
  63.1 1.2 collective-permute-start.1
  64.4 0.8 slice.79
  65.2 1.6 fusion
  67.4 0.6 constant_dynamic-update-slice_fusion.6
  68.7 0.6 constant_dynamic-update-slice_fusion.4
  70.0 46.6 %pass1.1 = (f32[4,256,1536]{2,1,0:T(8,128)}, f32[4,16,256]{2,1,0:T(8,128)}, bf16[10,256,512]{2,1,0:T(8,128)(2,1)}, bf16[10,256,1024]{2,1,0:T(8,128)(2,1)}) custom-call(s32[40]{0:T(128)} %reshape.63.hot_ref, s32[1]{0:T(128)} %bitcast.ep_ref, bf16[10,1536,512]{2,1,0:T(8,128)(2,1)} %w1_ref.3, bf16[10,1536,512]{2,1,0:T(8,128)(2,1)} %w3_ref.3, ...), custom_call_target="tpu_custom_call" | custom-call | flops 40000000000 | bytes 100000000 | tf_op jit(solution)/shard_map/pass1/pallas_call | solution.py:416
  116.6 1.3 constant_dynamic-update-slice_fusion.3
  118.0 1.3 constant_dynamic-update-slice_fusion.2
  119.3 0.8 slice.80
  120.1 0.6 constant_dynamic-update-slice_fusion.1
  120.7 13.4 %back.1 = (bf16[2,640,1536]{2,1,0:T(8,128)(2,1)}, bf16[2,96,1536]{2,1,0:T(8,128)(2,1)}, bf16[2,640,1536]{2,1,0:T(8,128)(2,1)}, bf16[2,96,1536]{2,1,0:T(8,128)(2,...) custom-call(bf16[256,1536]{1,0:T(8,128)(2,1)} %collective-permute-do, ...), custom_call_target="tpu_custom_call" | custom-call | flops 8000000000 | bytes 50000000 | tf_op jit(solution)/shard_map/back/pallas_call | solution.py:453
  134.1 0.8 slice.76
  135.0 0.6 constant_dynamic-update-slice_fusion
  135.6 1.0 reduce_max.19
  137.5 81.7 %pass2.1 = (f32[10,1536,512]{2,1,0:T(8,128)}, f32[10,1536,512]{2,1,0:T(8,128)}, f32[10,512,1536]{2,1,0:T(8,128)}) custom-call(s32[80]{0:T(128)} %reshape.65.hot_ref, bf16[10,1536,512]{2,1,0:T(8,128)(2,1)} %w1_ref.3, bf16[10,1536,512]{2,1,0:T(8,128)(2,1)} %w3_ref.3, bf16[10,512,1536]{2,1,0:T(8,128)(2,1)} %w2_ref.3, ...), custom_call_target="tpu_custom_call" | custom-call | flops 60000002048 | bytes 200000000 | tf_op jit(solution)/shard_map/pass2/pallas_call | solution.py:493
  219.2 6.4 %finish.1 = (bf16[256,1536]{1,0:T(8,128)(2,1)}, f32[64,1536]{1,0:T(8,128)}) custom-call(s32[1]{0:T(128)} %bitcast.ep_ref, f32[256,1536]{1,0:T(8,128)} %get-tuple-element.43.keep_ref, f32[256,1536]{1,0:T(8,128)} %collective-permute-done.3.far_ref, bf16[64,1536]{1,0:T(8,128)(2,1)} %bitcast.42, bf16[256,1536]{1,0:T(8,128)(2,1)} %x0_ref.1, ...), custom_call_target="tpu_custom_call" | custom-call | flops 4000000000 | bytes 10000000 | tf_op jit(solution)/shard_map/finish/pallas_call | solution.py:532
  225.6 1.7 reshape.61
  (17 shorter events, 3.2 us)
Async XLA Ops:
  59.6 59.7 %collective-permute-start.2 = (f32[2,4,16,256]{3,2,1,0:T(8,128)}, f32[2,4,16,256]{3,2,1,0:T(8,128)}, u32[]{:S(2)}, u32[]{:S(2)}) collective-permute-start(f32[2,4,16,256]{3,2,1,0:T(8,128)} %get-tuple-element.74.refs_2_), channel_id=1, source_target_pairs={{0,4},{1,5},{2,6},{3,7},{4,0},{5,1},{6,2},{7,3}} | collective-permute-start | bytes 393224 | tf_op jit(solution)/shard_map/ppermute | solution.py:345
  62.9 57.8 %collective-permute-start = (bf16[256,1536]{1,0:T(8,128)(2,1)}, bf16[256,1536]{1,0:T(8,128)(2,1)}, u32[]{:S(2)}, u32[]{:S(2)}) collective-permute-start(bf16[256,1536]{1,0:T(8,128)(2,1)} %slice_bitcast_fusion), channel_id=1, source_target_pairs={{0,4},{1,5},{2,6},{3,7},{4,0},{5,1},{6,2},{7,3}} | collective-permute-start | bytes 2359304 | tf_op jit(solution)/shard_map/ppermute | solution.py:345
  63.1 57.6 %collective-permute-start.1 = (bf16[256,1536]{1,0:T(8,128)(2,1)}, bf16[256,1536]{1,0:T(8,128)(2,1)}, u32[]{:S(2)}, u32[]{:S(2)}) collective-permute-start(bf16[256,1536]{1,0:T(8,128)(2,1)} %get-tuple-element.33), channel_id=1, source_target_pairs={{0,4},{1,5},{2,6},{3,7},{4,0},{5,1},{6,2},{7,3}} | collective-permute-start | bytes 2359304 | tf_op jit(solution)/shard_map/ppermute | solution.py:345
  137.3 82.0 %collective-permute-start.3 = (f32[256,1536]{1,0:T(8,128)}, f32[256,1536]{1,0:T(8,128)}, u32[]{:S(2)}, u32[]{:S(2)}) collective-permute-start(f32[256,1536]{1,0:T(8,128)} %get-tuple-element.44), channel_id=1, source_target_pairs={{0,2},{1,3},{2,0},{3,1},{4,6},{5,7},{6,4},{7,5}} | collective-permute-start | bytes 4718600 | tf_op jit(solution)/shard_map/ppermute | solution.py:345
where the time goes:
time: 228 us; the launch traced here: 227 us
  Pallas kernels  204 us (89%)
  local copies, waits for them, and re-layouts  19 us (8%)
  starting transfers between devices  2.97 us (1%)
    pallas_call x1, Pallas kernels, device_step(): pl.pallas_call(functools.partial(pass2_kernel, ep), out_shape=[jax.ShapeD...  81.7 us
    pallas_call x1, Pallas kernels, device_step(): pl.pallas_call(functools.partial(near_kernel, n_loc), out_shape=[sds((6,...  53.2 us
    pallas_call x1, Pallas kernels, device_step(): pl.pallas_call(functools.partial(pass1_kernel, ep, n_loc), out_shape=[jax...  46.6 us
    pallas_call x1, Pallas kernels, device_step(): pl.pallas_call(functools.partial(back_kernel, n_loc), out_shape=[sds((2,...  13.4 us
    pallas_call x1, Pallas kernels, device_step(): pl.pallas_call(functools.partial(finish_kernel, ep), out_shape=[jax.Shape...  6.39 us
    unnamed x7, local copies, waits for them, and re-layouts  5.64 us
  transfers between devices with their start and end apart: 4, of which 0 were waited for; matrix products, arithmetic and copies ran while one was open for 5% of the time, Pallas kernels for 56%

commit v1 on v0

v1 whole, which is shorter than its diff:
```python
import functools

import jax
import jax.numpy as jnp
from jax import lax
from jax.experimental import pallas as pl
from jax.experimental.pallas import tpu as pltpu
from jax.sharding import PartitionSpec as P

SLOTS = 64
EXTRA = 96
PAD = 16
F32 = jnp.float32
BF16 = jnp.bfloat16
VMEM_LIMIT = 67043328
MESH = pl.DeviceIdType.MESH


def nt_dot(a, b):
    return lax.dot_general(a, b, (((1,), (1,)), ((), ())), preferred_element_type=F32)


def tn_dot(a, b):
    return lax.dot_general(a, b, (((0,), (0,)), ((), ())), preferred_element_type=F32)


def nn_dot(a, b):
    return jnp.dot(a, b, preferred_element_type=F32)


def slot_mask(rank_row, rows, first):
    slot = lax.broadcasted_iota(jnp.int32, (rows, rank_row.shape[1]), 0) + first
    return slot.astype(F32) == rank_row


def hot_rows(rank):
    return jnp.max(rank, axis=1, keepdims=True) >= SLOTS


def extra_rank(rank):
    return jnp.max(jnp.where(hot_rows(rank), rank, -1.0), axis=0, keepdims=True)


def route_kernel(groups, per_group, x_ref, wr_ref, idx_ref, out_ref):
    rows, toks = groups * PAD, x_ref.shape[0]
    logits = nt_dot(wr_ref[...], x_ref[...])
    row = lax.broadcasted_iota(jnp.int32, (rows, toks), 0)
    expert = jnp.where(row % PAD < per_group, (row // PAD) * per_group + row % PAD, -1)
    chosen = expert == idx_ref[0:1, :]
    for k in range(1, idx_ref.shape[0]):
        chosen = chosen | (expert == idx_ref[k : k + 1, :])
    before = lax.broadcasted_iota(jnp.int32, (toks, toks), 0) < lax.broadcasted_iota(jnp.int32, (toks, toks), 1)
    rank = nn_dot(chosen.astype(F32).astype(BF16), before.astype(F32).astype(BF16))
    top = jnp.max(jnp.where(chosen, logits, -jnp.inf), axis=0, keepdims=True)
    weight = jnp.where(chosen, jnp.exp(logits - top), 0.0)
    prob = weight / jnp.sum(weight, axis=0, keepdims=True)
    out_ref[0] = jnp.where(chosen, rank, -1.0).reshape(groups, PAD, toks)
    out_ref[1] = prob.reshape(groups, PAD, toks)


def gather_rows(me, per_group, m_ref, x_ref, g_ref, x_out, d_out, g_out):
    step = per_group // 2

    def emit(masks, probs, where):
        pick = jnp.concatenate([m.astype(F32).astype(BF16) for m in masks], axis=0)
        gate = jnp.concatenate([jnp.sum(jnp.where(m, p, 0.0), axis=1, keepdims=True) for m, p in zip(masks, probs)], axis=0)
        x_out[where, :] = nn_dot(pick, x_ref[...]).astype(BF16)
        rows_g = nn_dot(pick, g_ref[...])
        if g_out is not None:
            g_out[where, :] = rows_g.astype(BF16)
        d_out[where, :] = (gate * rows_g).astype(BF16)

    def part(i, carry):
        ranks = [m_ref[0, me, pl.ds(i * step + k, 1), :] for k in range(step)]
        probs = [m_ref[1, me, pl.ds(i * step + k, 1), :] for k in range(step)]
        emit([slot_mask(r, SLOTS, 0) for r in ranks], probs, pl.ds(pl.multiple_of(i * (step * SLOTS), SLOTS), step * SLOTS))
        return carry

    lax.fori_loop(0, 2, part, 0)
    rank, prob = m_ref[0, me], m_ref[1, me]
    prob_hot = jnp.sum(jnp.where(hot_rows(rank), prob, 0.0), axis=0, keepdims=True)
    emit([slot_mask(extra_rank(rank), EXTRA, SLOTS)], [prob_hot], pl.ds(per_group * SLOTS, EXTRA))


class Stage:
    def __init__(self, main, bufs, sems, outs):
        self.main, self.bufs, self.sems, self.outs, self.busy, self.turn = main, bufs, sems, outs, {}, 0

    def gather(self, i, kinds, me, per_group, m_ref, x_ref, g_ref):
        slot, self.turn = self.turn, 1 - self.turn
        self.drain(slot)
        views = [self.bufs[k].at[slot] for k in range(kinds)]
        gather_rows(me, per_group, m_ref, x_ref, g_ref, *(views + [None])[:3])
        copies = []
        for k in range(kinds):
            copies.append(pltpu.make_async_copy(views[k].at[pl.ds(0, self.main)], self.outs[2 * k].at[i], self.sems.at[slot, 2 * k]))
            copies.append(pltpu.make_async_copy(views[k].at[pl.ds(self.main, EXTRA)], self.outs[2 * k + 1].at[i], self.sems.at[slot, 2 * k + 1]))
        for c in copies:
            c.start()
        self.busy[slot] = copies

    def drain(self, slot):
        for c in self.busy.pop(slot, ()):
            c.wait()


def device_of(bit):
    return (lax.axis_index("dp") ^ (bit >> 2), lax.axis_index("ep") ^ (bit & 3))


def greet(bits):
    barrier = pltpu.get_barrier_semaphore()
    for bit in bits:
        pl.semaphore_signal(barrier, inc=1, device_id=device_of(bit), device_id_type=MESH)
    pl.semaphore_wait(barrier, len(bits))


def near_kernel(per_group, x_ref, g_ref, m_ref, *refs):
    rows_out, (xs_out, ms_out, hot_out) = refs[:6], refs[6:9]
    x_in, g_in, m_in, st_x, st_d, st_g, send, recv, out_sem, st_sem = refs[9:]
    me = lax.axis_index("ep")
    greet((1, 2, 4))
    own = (x_ref, g_ref, m_ref)
    land = lambda s: own if s == 0 else (x_in.at[s - 1], g_in.at[s - 1], m_in.at[s - 1])
    flights = {}

    def push(k, source, s, bit):
        c = pltpu.make_async_remote_copy(src_ref=land(source)[k], dst_ref=land(s)[k], send_sem=send.at[s - 1, k], recv_sem=recv.at[s - 1, k], device_id=device_of(bit), device_id_type=MESH)
        c.start()
        flights[s, k] = c

    outs = []

    def keep(k, s):
        out = xs_out if k == 0 else ms_out
        c = pltpu.make_async_copy(land(s)[k], out.at[s - 1], out_sem.at[s - 1, k // 2])
        c.start()
        outs.append(c)

    def arrive(k, s, *onward):
        flights[s, k].wait_recv()
        for to, bit in onward:
            push(k, s, to, bit)
        if k != 1:
            keep(k, s)

    stage = Stage(per_group * SLOTS, (st_x, st_d, st_g), st_sem, rows_out)

    def gather(s):
        x, g, m = land(s)
        stage.gather(s, 3 if s < 4 else 2, me, per_group, m, x, g)
        hot = hot_rows(m[0, me]).astype(jnp.int32)
        shape = (hot.shape[0], hot_out.shape[1])
        diagonal = lax.broadcasted_iota(jnp.int32, shape, 0) == lax.broadcasted_iota(jnp.int32, shape, 1)
        hot_out[s : s + 1, :] = jnp.sum(jnp.where(diagonal, hot, 0), axis=0, keepdims=True)

    X, G, M = range(3)
    for k in (X, G, M):
        push(k, 0, 2, 2)
    for k in (G, X, M):
        push(k, 0, 4, 4)
    for k in (X, G, M):
        push(k, 0, 1, 1)
    gather(0)
    for k in (X, G, M):
        arrive(k, 1)
    gather(1)
    arrive(X, 2, (6, 4), (3, 1))
    arrive(G, 4, (6, 2), (5, 1))
    arrive(G, 2, (3, 1))
    arrive(M, 2, (6, 4), (3, 1))
    arrive(X, 4, (5, 1))
    arrive(M, 4, (5, 1))
    gather(2)
    gather(4)
    for s in (3, 5):
        for k in (X, G, M):
            arrive(k, s)
        gather(s)
    for k in (X, G, M):
        arrive(k, 6, (7, 1))
    gather(6)
    for k in (X, G, M):
        arrive(k, 7)
    gather(7)
    stage.drain(0)
    stage.drain(1)
    for c in flights.values():
        c.wait_send()
    for c in outs:
        c.wait()


def back_kernel(q_ref, gx_ref, me_ref, peer_ref, q_out, part_in, q_in, send, recv, q_send, q_recv, ld_sem):
    n_dev = q_in.shape[0]
    greet(tuple(range(1, n_dev)))

    def push(src, dst, i, bit, s_sem, r_sem):
        c = pltpu.make_async_remote_copy(src_ref=src, dst_ref=dst, send_sem=s_sem.at[i], recv_sem=r_sem.at[i], device_id=device_of(bit), device_id_type=MESH)
        c.start()
        return c

    parts = {h: push(gx_ref.at[2 * h + 1], part_in.at[h], h, 1, send, recv) for h in (1, 0)}
    qs = [push(q_ref, q_in.at[bit], bit, bit, q_send, q_recv) for bit in range(1, n_dev)]
    loads = [pltpu.make_async_copy(gx_ref.at[2 * h], dst, ld_sem.at[h]) for h, dst in enumerate((me_ref, peer_ref))]
    for c in loads:
        c.start()
    q_out[0] = q_ref[...]
    for i, c in enumerate(qs):
        c.wait_recv()
        q_out[i + 1] = q_in[i + 1]
    for h, dst in ((1, peer_ref), (0, me_ref)):
        loads[h].wait()
        parts[h].wait_recv()
        dst[...] += part_in[h]
    for c in qs + list(parts.values()):
        c.wait_send()


def expert_math(x, d, w1, w3, w2):
    z1 = nn_dot(x, w1)
    z3 = nn_dot(x, w3)
    sig = jax.nn.sigmoid(z1)
    silu = z1 * sig
    act = (silu * z3).astype(BF16)
    d_act = nt_dot(d, w2)
    dz1 = (d_act * z3 * sig * (1.0 + z1 * (1.0 - sig))).astype(BF16)
    dz3 = (d_act * silu).astype(BF16)
    return act, dz1, dz3


def flat(ref, first=0, count=None):
    v = ref[first : first + (count or ref.shape[0])]
    return v.reshape(v.shape[0] * v.shape[1], v.shape[2])


def pass1_kernel(per_group, hot_ref, ep_ref, w1_ref, w3_ref, w2_ref, x_ref, d_ref, g_ref, xo_ref, do_ref, go_ref, m0_ref, ms_ref, gx_ref, q_ref, act_ref, dz_ref, acto_ref, dzo_ref, r_scr):
    n_sh, n_all = g_ref.shape[0], x_ref.shape[0]
    e = pl.program_id(0)
    ff = w1_ref.shape[2]
    w1, w3, w2 = w1_ref[0], w3_ref[0], w2_ref[0]
    base = per_group * SLOTS
    m_of = lambda j: m0_ref.at[0, 0] if j == 0 else ms_ref.at[j - 1, 0, 0]

    def token_math(act, dz1, dz3, g):
        q = jnp.sum(nn_dot(act, w2) * g.astype(F32), axis=1, keepdims=True)
        return q, (nt_dot(dz1, w1) + nt_dot(dz3, w3)).astype(BF16)

    @pl.when(e == 0)
    def _():
        r_scr[:, base : base + EXTRA, :] = jnp.zeros((n_sh, EXTRA, r_scr.shape[2]), BF16)
        q_ref[...] = jnp.zeros_like(q_ref)
        acto_ref[...] = jnp.zeros_like(acto_ref)
        dzo_ref[...] = jnp.zeros_like(dzo_ref)

    act, dz1, dz3 = expert_math(flat(x_ref), flat(d_ref), w1, w3, w2)
    act_ref[0] = act
    dz_ref[0, :, :ff] = dz1
    dz_ref[0, :, ff:] = dz3
    near = n_sh * SLOTS
    q, r = token_math(act[:near], dz1[:near], dz3[:near], flat(g_ref))
    for j in range(n_sh):
        mask = slot_mask(m_of(j)[pl.ds(e, 1), :], SLOTS, 0)
        q_ref[j, pl.ds(e, 1), :] = jnp.sum(jnp.where(mask, q[j * SLOTS : (j + 1) * SLOTS], 0.0), axis=0, keepdims=True)
        r_scr[j, pl.ds(pl.multiple_of(e * SLOTS, SLOTS), SLOTS), :] = r[j * SLOTS : (j + 1) * SLOTS]

    for first in range(0, n_all, n_sh):
        is_hot = [hot_ref[first + j, e] for j in range(n_sh)]

        @pl.when(sum(is_hot) > 0)
        def _():
            act, dz1, dz3 = expert_math(flat(xo_ref, first, n_sh), flat(do_ref, first, n_sh), w1, w3, w2)
            if first == 0:
                q, r = token_math(act, dz1, dz3, flat(go_ref))
            for j in range(n_sh):
                rows = slice(j * EXTRA, (j + 1) * EXTRA)

                @pl.when(is_hot[j] > 0)
                def _():
                    acto_ref[first + j] = act[rows]
                    dzo_ref[first + j, :, :ff] = dz1[rows]
                    dzo_ref[first + j, :, ff:] = dz3[rows]
                    if first == 0:
                        mask = slot_mask(m_of(j)[pl.ds(e, 1), :], EXTRA, SLOTS)
                        q_ref[j, pl.ds(e, 1), :] += jnp.sum(jnp.where(mask, q[rows], 0.0), axis=0, keepdims=True)
                        r_scr[j, base : base + EXTRA, :] = r[rows]

    @pl.when(e == per_group - 1)
    def _():
        for j in range(n_sh):
            rank = m_of(j)[...]
            masks = [slot_mask(rank[i : i + 1, :], SLOTS, 0) for i in range(per_group)]
            masks.append(slot_mask(extra_rank(rank), EXTRA, SLOTS))
            pick = jnp.concatenate([m.astype(F32).astype(BF16) for m in masks], axis=0)
            gx_ref[j] = tn_dot(pick, r_scr[j])


def pass2_kernel(hot_ref, act_ref, dz_ref, x_ref, d_ref, xo_ref, do_ref, acto_ref, dzo_ref, g1_ref, g3_ref, g2_ref):
    n_all = x_ref.shape[0]
    e = pl.program_id(0)
    ff = g1_ref.shape[2]
    x = flat(x_ref)
    g1_ref[0] = tn_dot(x, dz_ref[0, :, :ff])
    g3_ref[0] = tn_dot(x, dz_ref[0, :, ff:])
    g2_ref[0] = tn_dot(act_ref[0], flat(d_ref))
    is_hot = [hot_ref[j, e] for j in range(n_all)]

    @pl.when(sum(is_hot) > 0)
    def _():
        keep = [h.astype(F32).astype(BF16) for h in is_hot]
        x = flat(xo_ref)
        dz = jnp.concatenate([dzo_ref[j] * keep[j] for j in range(n_all)], axis=0)
        d = jnp.concatenate([do_ref[j] * keep[j] for j in range(n_all)], axis=0)
        g1_ref[0] += tn_dot(x, dz[:, :ff])
        g3_ref[0] += tn_dot(x, dz[:, ff:])
        g2_ref[0] += tn_dot(flat(acto_ref), d)


def finish_kernel(groups, ep_ref, keep_ref, far_ref, wr_ref, x0_ref, xs_ref, m0_ref, ms_ref, q_ref, gx_ref, gr_ref):
    n_sh = q_ref.shape[0]
    x_refs = [x0_ref] + [xs_ref.at[i] for i in range(n_sh - 1)]
    m_refs = [m0_ref] + [ms_ref.at[i] for i in range(n_sh - 1)]
    ep = ep_ref[0]
    for s in range(n_sh):
        d, j = divmod(s, groups)
        q = jnp.concatenate([q_ref[d * groups + (ep ^ a), (ep ^ a) ^ j] for a in range(groups)], axis=0)
        p = m_refs[s][1].reshape(groups * PAD, q.shape[1])
        dl = p * (q - jnp.sum(p * q, axis=0, keepdims=True))
        dl = dl.astype(BF16)
        term = nn_dot(dl, x_refs[s][...])
        if s == 0:
            du = tn_dot(dl, wr_ref[...])
            gx_ref[...] = (keep_ref[...] + far_ref[...] + du).astype(BF16)
            gr_ref[...] = term
        else:
            gr_ref[...] += term


def solution(mesh):
    dp, ep = mesh.shape["dp"], mesh.shape["ep"]
    n_dev = dp * ep
    tok_spec = P(("dp", "ep"), None)
    exp_spec = P("ep", None, None)

    def swap(v, bit):
        return lax.ppermute(v, ("dp", "ep"), [(s, s ^ bit) for s in range(n_dev)])

    def device_step(x_loc, route_idx, w_router, w_gate, w_up, w_down, dy_loc):
        toks, dim = x_loc.shape
        n_exp = w_router.shape[1]
        n_loc, _, ff = w_gate.shape
        me = lax.axis_index("ep")
        ep_arr = me.reshape(1).astype(jnp.int32)
        vmem = pl.BlockSpec(memory_space=pltpu.VMEM)
        params = pltpu.CompilerParams(vmem_limit_bytes=VMEM_LIMIT)

        wr_rows = jnp.pad(w_router.T.reshape(ep, n_loc, dim), ((0, 0), (0, PAD - n_loc), (0, 0))).reshape(ep * PAD, dim)
        route = pl.pallas_call(
            functools.partial(route_kernel, ep, n_loc),
            out_shape=jax.ShapeDtypeStruct((2, ep, PAD, toks), F32),
            in_specs=[vmem] * 3,
            out_specs=vmem,
            compiler_params=params,
            cost_estimate=pl.CostEstimate(flops=10**9, bytes_accessed=10**6, transcendentals=0),
            name="route",
        )(x_loc, wr_rows, route_idx.T)

        hbm = pl.BlockSpec(memory_space=pl.ANY)
        main = n_loc * SLOTS
        sds = jax.ShapeDtypeStruct
        m_shape = route.shape
        others = n_dev - 1
        x_rows, x_more, d_rows, d_more, g_rows, g_more, xs, ms, hot = pl.pallas_call(
            functools.partial(near_kernel, n_loc),
            out_shape=[
                sds((n_dev, main, dim), BF16),
                sds((n_dev, EXTRA, dim), BF16),
                sds((n_dev, main, dim), BF16),
                sds((n_dev, EXTRA, dim), BF16),
                sds((ep, main, dim), BF16),
                sds((ep, EXTRA, dim), BF16),
                sds((others, toks, dim), BF16),
                sds((others,) + m_shape, F32),
                sds((n_dev, 128), jnp.int32),
            ],
            in_specs=[vmem] * 3,
            out_specs=[hbm] * 8 + [vmem],
            scratch_shapes=[
                pltpu.VMEM((others, toks, dim), BF16),
                pltpu.VMEM((others, toks, dim), BF16),
                pltpu.VMEM((others,) + m_shape, F32),
                pltpu.VMEM((2, main + EXTRA, dim), BF16),
                pltpu.VMEM((2, main + EXTRA, dim), BF16),
                pltpu.VMEM((2, main + EXTRA, dim), BF16),
                pltpu.SemaphoreType.DMA((others, 3)),
                pltpu.SemaphoreType.DMA((others, 3)),
                pltpu.SemaphoreType.DMA((others, 2)),
                pltpu.SemaphoreType.DMA((2, 6)),
            ],
            compiler_params=pltpu.CompilerParams(collective_id=0, has_side_effects=True, vmem_limit_bytes=VMEM_LIMIT),
            cost_estimate=pl.CostEstimate(flops=2 * 10**10, bytes_accessed=5 * 10**7, transcendentals=0),
            name="near",
        )(x_loc, dy_loc, route)

        w_specs = lambda im: [pl.BlockSpec((1, dim, ff), im), pl.BlockSpec((1, dim, ff), im), pl.BlockSpec((1, ff, dim), im)]
        im3 = lambda e, hot, ep_ref: (e, 0, 0)
        rows_at = lambda e, hot, ep_ref: (0, e, 0)
        fix = lambda shape: pl.BlockSpec(shape, lambda e, hot, ep_ref: (0,) * len(shape), pipeline_mode=pl.Buffered(1))
        n_row = n_dev * SLOTS
        gx_part, q_loc, act, dz, act_more, dz_more = pl.pallas_call(
            functools.partial(pass1_kernel, n_loc),
            out_shape=[
                sds((ep, toks, dim), F32),
                sds((ep, PAD, toks), F32),
                sds((n_loc, n_row, ff), BF16),
                sds((n_loc, n_row, 2 * ff), BF16),
                sds((n_dev, EXTRA, ff), BF16),
                sds((n_dev, EXTRA, 2 * ff), BF16),
            ],
            grid_spec=pltpu.PrefetchScalarGridSpec(
                num_scalar_prefetch=2,
                grid=(n_loc,),
                in_specs=w_specs(im3)
                + [pl.BlockSpec((n_dev, SLOTS, dim), rows_at)] * 2
                + [pl.BlockSpec((ep, SLOTS, dim), rows_at)]
                + [fix((n_dev, EXTRA, dim))] * 2
                + [fix((ep, EXTRA, dim))]
                + [pl.BlockSpec((1, 1, PAD, toks), lambda e, hot, ep_ref: (0, ep_ref[0], 0, 0))]
                + [pl.BlockSpec((ep - 1, 1, 1, PAD, toks), lambda e, hot, ep_ref: (0, 0, ep_ref[0], 0, 0))],
                out_specs=[fix((ep, toks, dim)), fix((ep, PAD, toks)), pl.BlockSpec((1, n_row, ff), im3), pl.BlockSpec((1, n_row, 2 * ff), im3)]
                + [fix((n_dev, EXTRA, ff)), fix((n_dev, EXTRA, 2 * ff))],
                scratch_shapes=[pltpu.VMEM((ep, main + EXTRA, dim), BF16)],
            ),
            compiler_params=params,
            cost_estimate=pl.CostEstimate(flops=4 * 10**10, bytes_accessed=10**8, transcendentals=0),
            name="pass1",
        )(hot, ep_arr, w_gate, w_up, w_down, x_rows, d_rows, g_rows, x_more, d_more, g_more, route, ms)

        for_me, for_peer, q_all = pl.pallas_call(
            back_kernel,
            out_shape=[sds((toks, dim), F32), sds((toks, dim), F32), sds((n_dev, ep, PAD, toks), F32)],
            in_specs=[vmem, hbm],
            out_specs=[vmem] * 3,
            scratch_shapes=[
                pltpu.VMEM((2, toks, dim), F32),
                pltpu.VMEM((n_dev, ep, PAD, toks), F32),
                pltpu.SemaphoreType.DMA((2,)),
                pltpu.SemaphoreType.DMA((2,)),
                pltpu.SemaphoreType.DMA((n_dev,)),
                pltpu.SemaphoreType.DMA((n_dev,)),
                pltpu.SemaphoreType.DMA((2,)),
            ],
            compiler_params=pltpu.CompilerParams(collective_id=1, has_side_effects=True, vmem_limit_bytes=VMEM_LIMIT),
            cost_estimate=pl.CostEstimate(flops=8 * 10**9, bytes_accessed=5 * 10**7, transcendentals=0),
            name="back",
        )(q_loc, gx_part)
        from_peer = swap(for_peer, 2)

        im3 = lambda e, hot: (e, 0, 0)
        rows_at = lambda e, hot: (0, e, 0)
        fix = lambda shape: pl.BlockSpec(shape, lambda e, hot: (0,) * len(shape), pipeline_mode=pl.Buffered(1))
        grad_gate, grad_up, grad_down = pl.pallas_call(
            pass2_kernel,
            out_shape=[sds((n_loc, dim, ff), F32), sds((n_loc, dim, ff), F32), sds((n_loc, ff, dim), F32)],
            grid_spec=pltpu.PrefetchScalarGridSpec(
                num_scalar_prefetch=1,
                grid=(n_loc,),
                in_specs=[pl.BlockSpec((1, n_row, ff), im3), pl.BlockSpec((1, n_row, 2 * ff), im3)]
                + [pl.BlockSpec((n_dev, SLOTS, dim), rows_at)] * 2
                + [fix((n_dev, EXTRA, dim))] * 2
                + [fix((n_dev, EXTRA, ff)), fix((n_dev, EXTRA, 2 * ff))],
                out_specs=w_specs(im3),
            ),
            compiler_params=params,
            cost_estimate=pl.CostEstimate(flops=6 * 10**10, bytes_accessed=2 * 10**8, transcendentals=0),
            name="pass2",
        )(hot, act, dz, x_rows, d_rows, x_more, d_more, act_more, dz_more)

        fixed = lambda shape: pl.BlockSpec(shape, lambda i, ep_ref: (0,) * len(shape))
        grad_x, grad_rt = pl.pallas_call(
            functools.partial(finish_kernel, ep),
            out_shape=[jax.ShapeDtypeStruct((toks, dim), BF16), jax.ShapeDtypeStruct((ep * PAD, dim), F32)],
            grid_spec=pltpu.PrefetchScalarGridSpec(
                num_scalar_prefetch=1,
                grid=(1,),
                in_specs=[fixed((toks, dim)), fixed((toks, dim)), fixed((ep * PAD, dim))]
                + [fixed(v.shape) for v in (x_loc, xs, route, ms, q_all)],
                out_specs=[fixed((toks, dim)), fixed((ep * PAD, dim))],
            ),
            compiler_params=params,
            cost_estimate=pl.CostEstimate(flops=4 * 10**9, bytes_accessed=10**7, transcendentals=0),
            name="finish",
        )(ep_arr, for_me, from_peer, wr_rows, x_loc, xs, route, ms, q_all)
        grad_router = grad_rt.reshape(ep, PAD, dim)[:, :n_loc].reshape(n_exp, dim).T
        return grad_x, grad_gate, grad_up, grad_down, grad_router

    return jax.shard_map(device_step, mesh=mesh, in_specs=(tok_spec, tok_spec, P(), exp_spec, exp_spec, exp_spec, tok_spec), out_specs=(tok_spec, exp_spec, exp_spec, exp_spec, P()), check_vma=False)
```

time: 228 us -> 215 us (0.943)
  the two profiles are of different devices: /device:TPU:3 before, /device:TPU:0 now
where the time goes in v1:
time: 215 us; the launch traced here: 213 us
  Pallas kernels  208 us (97%)
  local copies, waits for them, and re-layouts  3.37 us (2%)
    pallas_call x1, Pallas kernels, device_step(): pl.pallas_call(functools.partial(near_kernel, n_loc), out_shape=[sds((n_d...  69.9 us
    pallas_call x1, Pallas kernels, device_step(): pl.pallas_call(functools.partial(pass1_kernel, n_loc), out_shape=[sds((ep...  57.8 us
    pallas_call x1, Pallas kernels, device_step(): pl.pallas_call(pass2_kernel, out_shape=[sds((n_loc, dim, ff), F32), sds((...  53.7 us
    pallas_call x1, Pallas kernels, device_step(): pl.pallas_call(back_kernel, out_shape=[sds((toks, dim), F32), sds((toks,...  18.3 us
    pallas_call x1, Pallas kernels, device_step(): pl.pallas_call(functools.partial(finish_kernel, ep), out_shape=[jax.Shape...  6.3 us
  transfers between devices with their start and end apart: 1, of which 0 were waited for; matrix products, arithmetic and copies ran while one was open for 0% of the time, Pallas kernels for 25%

profile of v1, /device:TPU:0, one launch (start us, length us, event | category | flops | bytes accessed | tf_op | source)
XLA Modules:
  0.0 212.9 jit_solution(14602780719960349525)
XLA Ops:
  0.6 0.9 reshape.26
  1.6 0.7 pad.4
  2.3 2.3 %route.1.m_ref.m0_ref = f32[2,4,16,256]{3,2,1,0:T(8,128)} custom-call(bf16[256,1536]{1,0:T(8,128)(2,1)} %x0_ref.1, bf16[64,1536]{1,0:T(8,128)(2,1)} %bitcast.9, s32[8,256]{1,0:T(8,128)} %bitcast.12), custom_call_target="tpu_custom_call" | custom-call | flops 1000000000 | bytes 1000000 | tf_op jit(solution)/shard_map/route/pallas_call | solution.py:358
  4.6 69.9 %near.1 = (bf16[8,640,1536]{2,1,0:T(8,128)(2,1)}, bf16[8,96,1536]{2,1,0:T(8,128)(2,1)}, bf16[8,640,1536]{2,1,0:T(8,128)(2,1)}, bf16[8,96,1536]{2,1,0:T(8,128)(2,...) custom-call(bf16[256,1536]{1,0:T(8,128)(2,1)} %x0_ref.1, ...), custom_call_target="tpu_custom_call" | custom-call | flops 20000000000 | bytes 50000000 | tf_op jit(solution)/shard_map/near/pallas_call | solution.py:373
  74.5 57.8 %pass1.1 = (f32[4,256,1536]{2,1,0:T(8,128)}, f32[4,16,256]{2,1,0:T(8,128)}, bf16[10,512,512]{2,1,0:T(8,128)(2,1)}, bf16[10,512,1024]{2,1,0:T(8,128)(2,1)}, bf16[...) custom-call(s32[8,128]{1,0:T(8,128)} %get-tuple-element.28.hot_ref, s32[1]{0:T(128)} %bitcast.ep_ref, ...), custom_call_target="tpu_custom_call" | custom-call | flops 40000000000 | bytes 100000000 | tf_op jit(solution)/shard_map/pass1/pallas_call | solution.py:410
  132.3 18.3 %back.1 = (f32[256,1536]{1,0:T(8,128)}, f32[256,1536]{1,0:T(8,128)}, f32[8,4,16,256]{3,2,1,0:T(8,128)}) custom-call(f32[4,16,256]{2,1,0:T(8,128)} %get-tuple-element.36.q_ref, f32[4,256,1536]{2,1,0:T(8,128)} %get-tuple-element.37.gx_ref), custom_call_target="tpu_custom_call" | custom-call | flops 8000000000 | bytes 50000000 | tf_op jit(solution)/shard_map/back/pallas_call | solution.py:439
  150.6 0.6 collective-permute-start
  151.2 53.7 %pass2.1 = (f32[10,1536,512]{2,1,0:T(8,128)}, f32[10,1536,512]{2,1,0:T(8,128)}, f32[10,512,1536]{2,1,0:T(8,128)}) custom-call(s32[8,128]{1,0:T(8,128)} %get-tuple-element.28.hot_ref, bf16[10,512,512]{2,1,0:T(8,128)(2,1)} %get-tuple-element.43.act_ref, bf16[10,512,1024]{2,1,0:T(8,128)(2,1)} %get-tuple-element.44.dz_ref, ...), custom_call_target="tpu_custom_call" | custom-call | flops 60000002048 | bytes 200000000 | tf_op jit(solution)/shard_map/pass2/pallas_call | solution.py:462
  204.9 0.0 collective-permute-done.far_ref
  204.9 6.3 %finish.1 = (bf16[256,1536]{1,0:T(8,128)(2,1)}, f32[64,1536]{1,0:T(8,128)}) custom-call(s32[1]{0:T(128)} %bitcast.ep_ref, f32[256,1536]{1,0:T(8,128)} %get-tuple-element.38.keep_ref, f32[256,1536]{1,0:T(8,128)} %collective-permute-done.far_ref, bf16[64,1536]{1,0:T(8,128)(2,1)} %bitcast.10, bf16[256,1536]{1,0:T(8,128)(2,1)} %x0_ref.1, ...), custom_call_target="tpu_custom_call" | custom-call | flops 4000000000 | bytes 10000000 | tf_op jit(solution)/shard_map/finish/pallas_call | solution.py:480
  211.2 1.7 reshape.29
Async XLA Ops:
  150.6 54.3 %collective-permute-start = (f32[256,1536]{1,0:T(8,128)}, f32[256,1536]{1,0:T(8,128)}, u32[]{:S(2)}, u32[]{:S(2)}) collective-permute-start(f32[256,1536]{1,0:T(8,128)} %get-tuple-element.39), channel_id=1, source_target_pairs={{0,2},{1,3},{2,0},{3,1},{4,6},{5,7},{6,4},{7,5}} | collective-permute-start | bytes 4718600 | tf_op jit(solution)/shard_map/ppermute | solution.py:346

commit v2 on v1

v2 whole, which is shorter than its diff:
```python
import functools

import jax
import jax.numpy as jnp
from jax import lax
from jax.experimental import pallas as pl
from jax.experimental.pallas import tpu as pltpu
from jax.sharding import PartitionSpec as P

SLOTS = 56
EXTRA = 104
SPAN = 64
TAIL = 112
PAD = 16
F32 = jnp.float32
BF16 = jnp.bfloat16
VMEM_LIMIT = 67043328
MESH = pl.DeviceIdType.MESH


def nt_dot(a, b):
    return lax.dot_general(a, b, (((1,), (1,)), ((), ())), preferred_element_type=F32)


def tn_dot(a, b):
    return lax.dot_general(a, b, (((0,), (0,)), ((), ())), preferred_element_type=F32)


def nn_dot(a, b):
    return jnp.dot(a, b, preferred_element_type=F32)


def slot_mask(rank_row, rows, first):
    slot = lax.broadcasted_iota(jnp.int32, (rows, rank_row.shape[1]), 0) + first
    return slot.astype(F32) == rank_row


def hot_rows(rank):
    return jnp.max(rank, axis=1, keepdims=True) >= SLOTS


def extra_rank(rank):
    return jnp.max(jnp.where(hot_rows(rank), rank, -1.0), axis=0, keepdims=True)


def route(per_group, x_ref, idx_ref, wr_ref, out_ref):
    groups, toks = out_ref.shape[1], x_ref.shape[0]
    logits = nn_dot(x_ref[...], wr_ref[...]).T
    expert = lax.broadcasted_iota(jnp.int32, logits.shape, 0)
    chosen = expert == idx_ref[0:1, :]
    for k in range(1, idx_ref.shape[0]):
        chosen = chosen | (expert == idx_ref[k : k + 1, :])
    before = lax.broadcasted_iota(jnp.int32, (toks, toks), 0) < lax.broadcasted_iota(jnp.int32, (toks, toks), 1)
    rank = nn_dot(chosen.astype(F32).astype(BF16), before.astype(F32).astype(BF16))
    top = jnp.max(jnp.where(chosen, logits, -jnp.inf), axis=0, keepdims=True)
    weight = jnp.where(chosen, jnp.exp(logits - top), 0.0)
    prob = weight / jnp.sum(weight, axis=0, keepdims=True)
    rank = jnp.where(chosen, rank, -1.0)
    for a in range(groups):
        rows = slice(a * per_group, (a + 1) * per_group)
        out_ref[0, a, :per_group, :] = rank[rows]
        out_ref[0, a, per_group:, :] = jnp.full((PAD - per_group, toks), -1.0, F32)
        out_ref[1, a, :per_group, :] = prob[rows]
        out_ref[1, a, per_group:, :] = jnp.zeros((PAD - per_group, toks), F32)


def gather_rows(me, per_group, m_refs, x_refs, g_refs, x_out, d_out, g_out):
    step = per_group // 2

    def emit(masks, probs, size, first):
        def put(out, pair):
            for k in range(len(masks[0])):
                rows = jnp.concatenate([v[k * size : (k + 1) * size] for v in pair], axis=0)
                start = first + k * (2 * size)
                out[pl.ds(start if isinstance(start, int) else pl.multiple_of(start, 16), 2 * size), :] = rows.astype(BF16)

        picks = [jnp.concatenate([m.astype(F32) for m in ms], axis=0).astype(BF16) for ms in masks]
        put(x_out, [nn_dot(pick, x[...]) for pick, x in zip(picks, x_refs)])
        rows_g = [nn_dot(pick, g[...]) for pick, g in zip(picks, g_refs)]
        if g_out is not None:
            put(g_out, rows_g)
        gates = [jnp.concatenate([jnp.sum(jnp.where(m, p, 0.0), axis=1, keepdims=True) for m, p in zip(*mp)], axis=0) for mp in zip(masks, probs)]
        put(d_out, [gate * v for gate, v in zip(gates, rows_g)])

    def part(i, carry):
        masks = [[slot_mask(m[0, me, pl.ds(i * step + k, 1), :], SLOTS, 0) for k in range(step)] for m in m_refs]
        probs = [[m[1, me, pl.ds(i * step + k, 1), :] for k in range(step)] for m in m_refs]
        emit(masks, probs, SLOTS, i * (step * 2 * SLOTS))
        return carry

    lax.fori_loop(0, 2, part, 0)
    masks, probs = [], []
    for m in m_refs:
        rank, prob = m[0, me], m[1, me]
        masks.append([slot_mask(extra_rank(rank), EXTRA, SLOTS)])
        probs.append([jnp.sum(jnp.where(hot_rows(rank), prob, 0.0), axis=0, keepdims=True)])
    emit(masks, probs, EXTRA, per_group * 2 * SLOTS)


class Stage:
    def __init__(self, main, bufs, sems, outs):
        self.main, self.bufs, self.sems, self.outs, self.busy, self.turn = main, bufs, sems, outs, {}, 0

    def gather(self, i, kinds, *args):
        slot, self.turn = self.turn, 1 - self.turn
        self.drain(slot)
        views = [self.bufs[k].at[slot] for k in range(kinds)]
        gather_rows(*args, *(views + [None])[:3])
        copies = []
        for k in range(kinds):
            copies.append(pltpu.make_async_copy(views[k].at[pl.ds(0, self.main)], self.outs[2 * k].at[i], self.sems.at[slot, 2 * k]))
            copies.append(pltpu.make_async_copy(views[k].at[pl.ds(self.main, 2 * EXTRA)], self.outs[2 * k + 1].at[i], self.sems.at[slot, 2 * k + 1]))
        for c in copies:
            c.start()
        self.busy[slot] = copies

    def drain(self, slot):
        for c in self.busy.pop(slot, ()):
            c.wait()


def device_of(bit):
    return (lax.axis_index("dp") ^ (bit >> 2), lax.axis_index("ep") ^ (bit & 3))


def greet(bits):
    barrier = pltpu.get_barrier_semaphore()
    for bit in bits:
        pl.semaphore_signal(barrier, inc=1, device_id=device_of(bit), device_id_type=MESH)
    pl.semaphore_wait(barrier, len(bits))


def near_kernel(per_group, x_ref, g_ref, idx_ref, wr_ref, *refs):
    rows_out, (xs_out, ms_out, hot_out) = refs[:6], refs[6:9]
    x_in, g_in, i_in, st_x, st_d, st_g, send, recv, out_sem, st_sem = refs[9:]
    me = lax.axis_index("ep")
    greet((1, 2, 4))
    own = (x_ref, g_ref, idx_ref)
    land = lambda s: own if s == 0 else (x_in.at[s - 1], g_in.at[s - 1], i_in.at[s - 1])
    flights = {}

    def push(k, source, s, bit):
        c = pltpu.make_async_remote_copy(src_ref=land(source)[k], dst_ref=land(s)[k], send_sem=send.at[s - 1, k], recv_sem=recv.at[s - 1, k], device_id=device_of(bit), device_id_type=MESH)
        c.start()
        flights[s, k] = c

    outs = []

    def arrive(k, s, *onward):
        flights[s, k].wait_recv()
        for to, bit in onward:
            push(k, s, to, bit)
        if k == 0:
            c = pltpu.make_async_copy(land(s)[k], xs_out.at[s - 1], out_sem.at[s - 1])
            c.start()
            outs.append(c)

    stage = Stage(per_group * 2 * SLOTS, (st_x, st_d, st_g), st_sem, rows_out)

    def routing(s):
        x, _, idx = land(s)
        route(per_group, x, idx, wr_ref, ms_out.at[s])
        hot = hot_rows(ms_out[s, 0, me]).astype(jnp.int32)
        shape = (hot.shape[0], hot_out.shape[1])
        diagonal = lax.broadcasted_iota(jnp.int32, shape, 0) == lax.broadcasted_iota(jnp.int32, shape, 1)
        hot_out[s : s + 1, :] = jnp.sum(jnp.where(diagonal, hot, 0), axis=0, keepdims=True)

    def gather(s):
        pair = (s, s + 1)
        stage.gather(s // 2, 3 if s < 4 else 2, me, per_group, [ms_out.at[i] for i in pair], [land(i)[0] for i in pair], [land(i)[1] for i in pair])

    X, G, I = range(3)
    for k in (X, I, G):
        push(k, 0, 2, 2)
    for k in (G, I, X):
        push(k, 0, 4, 4)
    for k in (X, I, G):
        push(k, 0, 1, 1)
    routing(0)
    for k in (X, G, I):
        arrive(k, 1)
    routing(1)
    gather(0)
    arrive(X, 2, (6, 4), (3, 1))
    arrive(I, 2, (6, 4), (3, 1))
    arrive(G, 4, (6, 2), (5, 1))
    arrive(I, 4, (5, 1))
    routing(2)
    arrive(X, 3)
    arrive(I, 3)
    routing(3)
    arrive(G, 2, (3, 1))
    arrive(X, 4, (5, 1))
    routing(4)
    arrive(G, 3)
    gather(2)
    for k in (X, G, I):
        arrive(k, 5)
    routing(5)
    gather(4)
    for k in (X, I, G):
        arrive(k, 6, (7, 1))
    routing(6)
    for k in (X, I, G):
        arrive(k, 7)
    routing(7)
    gather(6)
    stage.drain(0)
    stage.drain(1)
    for c in flights.values():
        c.wait_send()
    for c in outs:
        c.wait()


def back_kernel(q_ref, keep_ref, give_ref, peer_ref, q_out, part_in, q_in, send, recv, q_send, q_recv, ld_sem):
    n_dev = q_in.shape[0]
    greet(tuple(range(1, n_dev)))

    def push(src, dst, bit, s_sem, r_sem):
        c = pltpu.make_async_remote_copy(src_ref=src, dst_ref=dst, send_sem=s_sem, recv_sem=r_sem, device_id=device_of(bit), device_id_type=MESH)
        c.start()
        return c

    part = push(give_ref, part_in, 1, send.at[0], recv.at[0])
    load = pltpu.make_async_copy(keep_ref, peer_ref, ld_sem.at[0])
    load.start()
    qs = [push(q_ref, q_in.at[bit], bit, q_send.at[bit], q_recv.at[bit]) for bit in range(1, n_dev)]
    q_out[0] = q_ref[...]
    load.wait()
    part.wait_recv()
    peer_ref[...] += part_in[...]
    for i, c in enumerate(qs):
        c.wait_recv()
        q_out[i + 1] = q_in[i + 1]
    for c in qs + [part]:
        c.wait_send()


def expert_math(x, d, w1, w3, w2):
    z1 = nn_dot(x, w1)
    z3 = nn_dot(x, w3)
    sig = jax.nn.sigmoid(z1)
    silu = z1 * sig
    act = (silu * z3).astype(BF16)
    d_act = nt_dot(d, w2)
    dz1 = (d_act * z3 * sig * (1.0 + z1 * (1.0 - sig))).astype(BF16)
    dz3 = (d_act * silu).astype(BF16)
    return act, dz1, dz3


def flat(ref, first=0, count=None):
    v = ref[first : first + (count or ref.shape[0])]
    return v.reshape(v.shape[0] * v.shape[1], v.shape[2])


def hot_column(is_hot):
    return jnp.concatenate([jnp.full((EXTRA, 1), 1.0, F32) * h.astype(F32) for h in is_hot], axis=0) > 0.0


def masked(column, v):
    return jnp.where(column, v.astype(F32), 0.0).astype(BF16)


def pass1_kernel(per_group, hot_ref, ep_ref, w1_ref, w3_ref, w2_ref, x_ref, d_ref, g_ref, xo_ref, do_ref, go_ref, ms_ref, *refs):
    n_pair = g_ref.shape[0]
    n_sh, n_all = 2 * n_pair, hot_ref.shape[0]
    gx_refs, (q_ref, act_ref, dz_ref, acto_ref, dzo_ref, r_scr) = refs[:n_sh], refs[n_sh:]
    e = pl.program_id(0)
    ff = w1_ref.shape[2]
    w1, w3, w2 = w1_ref[0], w3_ref[0], w2_ref[0]
    base = per_group * SPAN
    m_of = lambda j: ms_ref.at[j, 0, 0]

    def token_math(act, dz1, dz3, g):
        q = jnp.sum(nn_dot(act, w2) * g.astype(F32), axis=1, keepdims=True)
        return q, nt_dot(dz1, w1) + nt_dot(dz3, w3)

    @pl.when(e == 0)
    def _():
        r_scr[:, base:, :] = jnp.zeros((n_sh, TAIL, r_scr.shape[2]), BF16)
        for i in range(per_group):
            r_scr[:, i * SPAN + SPAN - 16 : (i + 1) * SPAN, :] = jnp.zeros((n_sh, 16, r_scr.shape[2]), BF16)
        acto_ref[...] = jnp.zeros_like(acto_ref)
        dzo_ref[...] = jnp.zeros_like(dzo_ref)

    act, dz1, dz3 = expert_math(flat(x_ref), flat(d_ref), w1, w3, w2)
    act_ref[0] = act
    dz_ref[0, :, :ff] = dz1
    dz_ref[0, :, ff:] = dz3
    near = n_sh * SLOTS
    q, r = token_math(act[:near], dz1[:near], dz3[:near], flat(g_ref))
    for j in range(n_sh):
        rows = slice(j * SLOTS, (j + 1) * SLOTS)
        mask = slot_mask(m_of(j)[pl.ds(e, 1), :], SLOTS, 0)
        q_ref[pl.ds(j * per_group + e, 1), :] = jnp.sum(jnp.where(mask, q[rows], 0.0), axis=0, keepdims=True)
        r_scr[j, pl.ds(pl.multiple_of(e * SPAN, SPAN), SLOTS), :] = r[rows].astype(BF16)

    for first in range(0, n_all, n_sh):
        is_hot = [hot_ref[first + j, e] for j in range(n_sh)]

        @pl.when(sum(is_hot) > 0)
        def _():
            part = first // 2
            column = hot_column(is_hot)
            d = masked(column, flat(do_ref, part, n_pair))
            act, dz1, dz3 = expert_math(flat(xo_ref, part, n_pair), d, w1, w3, w2)
            shape = (n_pair, 2 * EXTRA, ff)
            acto_ref[part : part + n_pair] += masked(column, act).reshape(shape)
            dzo_ref[part : part + n_pair, :, :ff] += dz1.reshape(shape)
            dzo_ref[part : part + n_pair, :, ff:] += dz3.reshape(shape)
            if first == 0:
                q, r = token_math(act, dz1, dz3, flat(go_ref))
                for j in range(n_sh):
                    rows = slice(j * EXTRA, (j + 1) * EXTRA)

                    @pl.when(is_hot[j] > 0)
                    def _():
                        mask = slot_mask(m_of(j)[pl.ds(e, 1), :], EXTRA, SLOTS)
                        q_ref[pl.ds(j * per_group + e, 1), :] += jnp.sum(jnp.where(mask, q[rows], 0.0), axis=0, keepdims=True)
                        r_scr[j, base : base + EXTRA, :] = r[rows].astype(BF16)

    @pl.when(e == per_group - 1)
    def _():
        for j in range(n_sh):
            rank = m_of(j)[...]
            low = jnp.where(rank < SLOTS, rank, -1.0)
            masks = [slot_mask(low[i : i + 1, :], SPAN, 0) for i in range(per_group)]
            masks.append(slot_mask(extra_rank(rank), TAIL, SLOTS))
            pick = jnp.concatenate([m.astype(F32) for m in masks], axis=0).astype(BF16)
            gx_refs[j][...] = tn_dot(pick, r_scr[j])


def pass2_kernel(hot_ref, act_ref, dz_ref, x_ref, d_ref, xo_ref, do_ref, acto_ref, dzo_ref, g1_ref, g3_ref, g2_ref):
    e = pl.program_id(0)
    ff = g1_ref.shape[2]
    x = flat(x_ref)
    g1_ref[0] = tn_dot(x, dz_ref[0, :, :ff])
    g3_ref[0] = tn_dot(x, dz_ref[0, :, ff:])
    g2_ref[0] = tn_dot(act_ref[0], flat(d_ref))
    is_hot = [hot_ref[j, e] for j in range(hot_ref.shape[0])]

    @pl.when(sum(is_hot) > 0)
    def _():
        column = hot_column(is_hot)
        x = flat(xo_ref)
        dz = masked(column, flat(dzo_ref))
        g1_ref[0] += tn_dot(x, dz[:, :ff])
        g3_ref[0] += tn_dot(x, dz[:, ff:])
        g2_ref[0] += tn_dot(flat(acto_ref), masked(column, flat(do_ref)))


def finish_kernel(per_group, ep_ref, own_ref, near_ref, far_ref, wr_ref, x0_ref, xs_ref, ms_ref, q_ref, gx_ref, gr_ref, acc):
    n_sh, groups = q_ref.shape[0], wr_ref.shape[0]
    ep = ep_ref[0]
    for s in range(n_sh):
        d, j = divmod(s, groups)
        rows = lambda m: slice((m ^ j) * per_group, ((m ^ j) + 1) * per_group)
        q = [q_ref[d * groups + m, rows(m), :] for m in range(groups)]
        p = [ms_ref[s, 0, ep ^ m][:per_group] for m in range(groups)]
        mean = sum(jnp.sum(a * b, axis=0, keepdims=True) for a, b in zip(p, q))
        gap = jnp.zeros((PAD - per_group, q[0].shape[1]), F32)
        dl = jnp.concatenate([v for a, b in zip(p, q) for v in (a * (b - mean), gap)], axis=0).astype(BF16)
        term = nn_dot(dl, x0_ref[...] if s == 0 else xs_ref[s - 1])
        if s == 0:
            wr = jnp.concatenate([wr_ref[ep ^ m] for m in range(groups)], axis=0)
            gx_ref[...] = (own_ref[...] + near_ref[...] + far_ref[...] + tn_dot(dl, wr)).astype(BF16)
            acc[...] = term
        else:
            acc[...] += term
    for m in range(groups):
        gr_ref[ep ^ m] = acc[m * PAD : (m + 1) * PAD, :]


def solution(mesh):
    dp, ep = mesh.shape["dp"], mesh.shape["ep"]
    n_dev = dp * ep
    tok_spec = P(("dp", "ep"), None)
    exp_spec = P("ep", None, None)

    def swap(v, bit):
        return lax.ppermute(v, ("dp", "ep"), [(s, s ^ bit) for s in range(n_dev)])

    def device_step(x_loc, route_idx, w_router, w_gate, w_up, w_down, dy_loc):
        toks, dim = x_loc.shape
        top_k = route_idx.shape[1]
        n_exp = w_router.shape[1]
        n_loc, _, ff = w_gate.shape
        me = lax.axis_index("ep")
        ep_arr = me.reshape(1).astype(jnp.int32)
        vmem = pl.BlockSpec(memory_space=pltpu.VMEM)
        params = pltpu.CompilerParams(vmem_limit_bytes=VMEM_LIMIT)

        wr_rows = jnp.pad(w_router.T.reshape(ep, n_loc, dim), ((0, 0), (0, PAD - n_loc), (0, 0)))
        m_shape = (2, ep, PAD, toks)
        hbm = pl.BlockSpec(memory_space=pl.ANY)
        main = n_loc * 2 * SLOTS
        pairs = n_dev // 2
        sds = jax.ShapeDtypeStruct
        others = n_dev - 1
        x_rows, x_more, d_rows, d_more, g_rows, g_more, xs, ms, hot = pl.pallas_call(
            functools.partial(near_kernel, n_loc),
            out_shape=[
                sds((pairs, main, dim), BF16),
                sds((pairs, 2 * EXTRA, dim), BF16),
                sds((pairs, main, dim), BF16),
                sds((pairs, 2 * EXTRA, dim), BF16),
                sds((ep // 2, main, dim), BF16),
                sds((ep // 2, 2 * EXTRA, dim), BF16),
                sds((others, toks, dim), BF16),
                sds((n_dev,) + m_shape, F32),
                sds((n_dev, 128), jnp.int32),
            ],
            in_specs=[vmem] * 4,
            out_specs=[hbm] * 7 + [vmem] * 2,
            scratch_shapes=[
                pltpu.VMEM((others, toks, dim), BF16),
                pltpu.VMEM((others, toks, dim), BF16),
                pltpu.VMEM((others, top_k, toks), jnp.int32),
                pltpu.VMEM((2, main + 2 * EXTRA, dim), BF16),
                pltpu.VMEM((2, main + 2 * EXTRA, dim), BF16),
                pltpu.VMEM((2, main + 2 * EXTRA, dim), BF16),
                pltpu.SemaphoreType.DMA((others, 3)),
                pltpu.SemaphoreType.DMA((others, 3)),
                pltpu.SemaphoreType.DMA((others,)),
                pltpu.SemaphoreType.DMA((2, 6)),
            ],
            compiler_params=pltpu.CompilerParams(collective_id=0, has_side_effects=True, vmem_limit_bytes=VMEM_LIMIT),
            cost_estimate=pl.CostEstimate(flops=2 * 10**10, bytes_accessed=5 * 10**7, transcendentals=0),
            name="near",
        )(x_loc, dy_loc, route_idx.T, w_router)

        w_specs = lambda im: [pl.BlockSpec((1, dim, ff), im), pl.BlockSpec((1, dim, ff), im), pl.BlockSpec((1, ff, dim), im)]
        im3 = lambda e, hot, ep_ref: (e, 0, 0)
        rows_at = lambda e, hot, ep_ref: (0, e, 0)
        fix = lambda shape: pl.BlockSpec(shape, lambda e, hot, ep_ref: (0,) * len(shape), pipeline_mode=pl.Buffered(1))
        n_row = n_dev * SLOTS
        *gx_part, q_loc, act, dz, act_more, dz_more = pl.pallas_call(
            functools.partial(pass1_kernel, n_loc),
            out_shape=[sds((toks, dim), F32)] * ep
            + [
                sds((ep * n_loc, toks), F32),
                sds((n_loc, n_row, ff), BF16),
                sds((n_loc, n_row, 2 * ff), BF16),
                sds((pairs, 2 * EXTRA, ff), BF16),
                sds((pairs, 2 * EXTRA, 2 * ff), BF16),
            ],
            grid_spec=pltpu.PrefetchScalarGridSpec(
                num_scalar_prefetch=2,
                grid=(n_loc,),
                in_specs=w_specs(im3)
                + [pl.BlockSpec((pairs, 2 * SLOTS, dim), rows_at)] * 2
                + [pl.BlockSpec((ep // 2, 2 * SLOTS, dim), rows_at)]
                + [fix((pairs, 2 * EXTRA, dim))] * 2
                + [fix((ep // 2, 2 * EXTRA, dim))]
                + [pl.BlockSpec((ep, 1, 1, PAD, toks), lambda e, hot, ep_ref: (0, 0, ep_ref[0], 0, 0))],
                out_specs=[fix((toks, dim))] * ep
                + [fix((ep * n_loc, toks)), pl.BlockSpec((1, n_row, ff), im3), pl.BlockSpec((1, n_row, 2 * ff), im3)]
                + [fix((pairs, 2 * EXTRA, ff)), fix((pairs, 2 * EXTRA, 2 * ff))],
                scratch_shapes=[pltpu.VMEM((ep, n_loc * SPAN + TAIL, dim), BF16)],
            ),
            compiler_params=params,
            cost_estimate=pl.CostEstimate(flops=4 * 10**10, bytes_accessed=10**8, transcendentals=0),
            name="pass1",
        )(hot, ep_arr, w_gate, w_up, w_down, x_rows, d_rows, g_rows, x_more, d_more, g_more, ms)

        from_core = swap(gx_part[1], 1)
        for_peer, q_all = pl.pallas_call(
            back_kernel,
            out_shape=[sds((toks, dim), F32), sds((n_dev, ep * n_loc, toks), F32)],
            in_specs=[vmem, hbm, hbm],
            out_specs=[vmem] * 2,
            scratch_shapes=[
                pltpu.VMEM((toks, dim), F32),
                pltpu.VMEM((n_dev, ep * n_loc, toks), F32),
                pltpu.SemaphoreType.DMA((1,)),
                pltpu.SemaphoreType.DMA((1,)),
                pltpu.SemaphoreType.DMA((n_dev,)),
                pltpu.SemaphoreType.DMA((n_dev,)),
                pltpu.SemaphoreType.DMA((1,)),
            ],
            compiler_params=pltpu.CompilerParams(collective_id=1, has_side_effects=True, vmem_limit_bytes=VMEM_LIMIT),
            cost_estimate=pl.CostEstimate(flops=8 * 10**9, bytes_accessed=5 * 10**7, transcendentals=0),
            name="back",
        )(q_loc, gx_part[2], gx_part[3])
        from_peer = swap(for_peer, 2)

        im3 = lambda e, hot: (e, 0, 0)
        rows_at = lambda e, hot: (0, e, 0)
        fix = lambda shape: pl.BlockSpec(shape, lambda e, hot: (0,) * len(shape), pipeline_mode=pl.Buffered(1))
        grad_gate, grad_up, grad_down = pl.pallas_call(
            pass2_kernel,
            out_shape=[sds((n_loc, dim, ff), F32), sds((n_loc, dim, ff), F32), sds((n_loc, ff, dim), F32)],
            grid_spec=pltpu.PrefetchScalarGridSpec(
                num_scalar_prefetch=1,
                grid=(n_loc,),
                in_specs=[pl.BlockSpec((1, n_row, ff), im3), pl.BlockSpec((1, n_row, 2 * ff), im3)]
                + [pl.BlockSpec((pairs, 2 * SLOTS, dim), rows_at)] * 2
                + [fix((pairs, 2 * EXTRA, dim))] * 2
                + [fix((pairs, 2 * EXTRA, ff)), fix((pairs, 2 * EXTRA, 2 * ff))],
                out_specs=w_specs(im3),
            ),
            compiler_params=params,
            cost_estimate=pl.CostEstimate(flops=6 * 10**10, bytes_accessed=2 * 10**8, transcendentals=0),
            name="pass2",
        )(hot, act, dz, x_rows, d_rows, x_more, d_more, act_more, dz_more)

        fixed = lambda shape: pl.BlockSpec(shape, lambda i, ep_ref: (0,) * len(shape))
        grad_x, grad_rt = pl.pallas_call(
            functools.partial(finish_kernel, n_loc),
            out_shape=[sds((toks, dim), BF16), sds((ep, PAD, dim), F32)],
            grid_spec=pltpu.PrefetchScalarGridSpec(
                num_scalar_prefetch=1,
                grid=(1,),
                in_specs=[fixed(v.shape) for v in (gx_part[0], from_core, from_peer, wr_rows, x_loc, xs)]
                + [pl.BlockSpec((n_dev, 1, ep, PAD, toks), lambda i, ep_ref: (0, 1, 0, 0, 0)), fixed(q_all.shape)],
                out_specs=[fixed((toks, dim)), fixed((ep, PAD, dim))],
                scratch_shapes=[pltpu.VMEM((ep * PAD, dim), F32)],
            ),
            compiler_params=params,
            cost_estimate=pl.CostEstimate(flops=4 * 10**9, bytes_accessed=10**7, transcendentals=0),
            name="finish",
        )(ep_arr, gx_part[0], from_core, from_peer, wr_rows, x_loc, xs, ms, q_all)
        grad_router = grad_rt[:, :n_loc].reshape(n_exp, dim).T
        return grad_x, grad_gate, grad_up, grad_down, grad_router

    return jax.shard_map(device_step, mesh=mesh, in_specs=(tok_spec, tok_spec, P(), exp_spec, exp_spec, exp_spec, tok_spec), out_specs=(tok_spec, exp_spec, exp_spec, exp_spec, P()), check_vma=False)
```

time: 215 us -> 208 us (0.967)
  Pallas kernels: 208 us -> 201 us
    pallas_call x5 -> x4, Pallas kernels: 155 us -> 146 us  [the longest x1 67.8 us: device_step(): pl.pallas_call(functools.partial(near_kernel, n_loc), out_shape=[sds((pai...]
  transfers between devices with their start and end apart: 1 -> 2, of which waited for: 0 -> 0; matrix products, arithmetic and copies ran while one was open for 0% -> 1% of each run, Pallas kernels for 25% -> 31%
where the time goes in v2:
time: 208 us; the launch traced here: 207 us
  Pallas kernels  201 us (97%)
  local copies, waits for them, and re-layouts  5.19 us (2%)
    pallas_call x1, Pallas kernels, device_step(): pl.pallas_call(functools.partial(near_kernel, n_loc), out_shape=[sds((pai...  67.8 us
    pallas_call x1, Pallas kernels, device_step(): pl.pallas_call(functools.partial(pass1_kernel, n_loc), out_shape=[sds((to...  62.3 us
    pallas_call x1, Pallas kernels, device_step(): pl.pallas_call(pass2_kernel, out_shape=[sds((n_loc, dim, ff), F32), sds((...  54.7 us
    pallas_call x1, Pallas kernels, device_step(): pl.pallas_call(back_kernel, out_shape=[sds((toks, dim), F32), sds((n_dev,...  9.46 us
    pallas_call x1, Pallas kernels, device_step(): pl.pallas_call(functools.partial(finish_kernel, n_loc), out_shape=[sds((t...  6.67 us
  transfers between devices with their start and end apart: 2, of which 0 were waited for; matrix products, arithmetic and copies ran while one was open for 1% of the time, Pallas kernels for 31%

profile of v2, /device:TPU:0, one launch (start us, length us, event | category | flops | bytes accessed | tf_op | source)
XLA Modules:
  0.0 207.4 jit_solution(11984740209506535374)
XLA Ops:
  0.6 1.8 copy.13.wr_ref
  2.5 67.8 %near.1 = (bf16[4,1120,1536]{2,1,0:T(8,128)(2,1)}, bf16[4,208,1536]{2,1,0:T(8,128)(2,1)}, bf16[4,1120,1536]{2,1,0:T(8,128)(2,1)}, bf16[4,208,1536]{2,1,0:T(8,128...) custom-call(bf16[256,1536]{1,0:T(8,128)(2,1)} %x0_ref.1, ...), custom_call_target="tpu_custom_call" | custom-call | flops 20000000000 | bytes 50000000 | tf_op jit(solution)/shard_map/near/pallas_call | solution.py:401
  70.2 62.3 %pass1.1 = (f32[256,1536]{1,0:T(8,128)}, f32[256,1536]{1,0:T(8,128)}, f32[256,1536]{1,0:T(8,128)}, f32[256,1536]{1,0:T(8,128)}, f32[40,256]{1,0:T(8,128)}, /*ind...) custom-call(s32[8,128]{1,0:T(8,128)} %get-tuple-element.30.hot_ref, ...), custom_call_target="tpu_custom_call" | custom-call | flops 40000000000 | bytes 100000000 | tf_op jit(solution)/shard_map/pass1/pallas_call | solution.py:438
  132.5 0.0 collective-permute-start
  132.6 9.5 %back.1 = (f32[256,1536]{1,0:T(8,128)}, f32[8,40,256]{2,1,0:T(8,128)}) custom-call(f32[40,256]{1,0:T(8,128)} %get-tuple-element.40.q_ref, f32[256,1536]{1,0:T(8,128)} %get-tuple-element.41.keep_ref, f32[256,1536]{1,0:T(8,128)} %get-tuple-element.42.give_ref), custom_call_target="tpu_custom_call" | custom-call | flops 8000000000 | bytes 50000000 | tf_op jit(solution)/shard_map/back/pallas_call | solution.py:468
  142.0 0.6 collective-permute-start.1
  142.6 54.7 %pass2.1 = (f32[10,1536,512]{2,1,0:T(8,128)}, f32[10,1536,512]{2,1,0:T(8,128)}, f32[10,512,1536]{2,1,0:T(8,128)}) custom-call(s32[8,128]{1,0:T(8,128)} %get-tuple-element.30.hot_ref, bf16[10,448,512]{2,1,0:T(8,128)(2,1)} %get-tuple-element.47.act_ref, bf16[10,448,1024]{2,1,0:T(8,128)(2,1)} %get-tuple-element.48.dz_ref, ...), custom_call_target="tpu_custom_call" | custom-call | flops 60000002048 | bytes 200000000 | tf_op jit(solution)/shard_map/pass2/pallas_call | solution.py:491
  197.4 0.9 reshape.20
  198.3 0.7 pad.4.wr_ref
  199.0 0.0 collective-permute-done.near_ref
  199.0 0.0 collective-permute-done.1.far_ref
  199.0 6.7 %finish.1 = (bf16[256,1536]{1,0:T(8,128)(2,1)}, f32[4,16,1536]{2,1,0:T(8,128)}) custom-call(s32[1]{0:T(128)} %bitcast.ep_ref, f32[256,1536]{1,0:T(8,128)} %get-tuple-element.38.own_ref, f32[256,1536]{1,0:T(8,128)} %collective-permute-done.near_ref, f32[256,1536]{1,0:T(8,128)} %collective-permute-done.1.far_ref, bf16[4,16,1536]{2,1,0:T(8,128)(2,1)} %pad.4.wr_ref, ...), custom_call_target="tpu_custom_call" | custom-call | flops 4000000000 | bytes 10000000 | tf_op jit(solution)/shard_map/finish/pallas_call | solution.py:509
  205.7 1.7 reshape.21
Async XLA Ops:
  132.5 66.5 %collective-permute-start = (f32[256,1536]{1,0:T(8,128)}, f32[256,1536]{1,0:T(8,128)}, u32[]{:S(2)}, u32[]{:S(2)}) collective-permute-start(f32[256,1536]{1,0:T(8,128)} %get-tuple-element.39), channel_id=1, source_target_pairs={{0,1},{1,0},{2,3},{3,2},{4,5},{5,4},{6,7},{7,6}} | collective-permute-start | bytes 4718600 | tf_op jit(solution)/shard_map/ppermute | solution.py:382
  142.0 57.0 %collective-permute-start.1 = (f32[256,1536]{1,0:T(8,128)}, f32[256,1536]{1,0:T(8,128)}, u32[]{:S(2)}, u32[]{:S(2)}) collective-permute-start(f32[256,1536]{1,0:T(8,128)} %get-tuple-element.43), channel_id=1, source_target_pairs={{0,2},{1,3},{2,0},{3,1},{4,6},{5,7},{6,4},{7,5}} | collective-permute-start | bytes 4718600 | tf_op jit(solution)/shard_map/ppermute | solution.py:382

commit v3 on v2

--- a/solution.py
+++ b/solution.py
@@ -45,7 +45,7 @@
 
 def route(per_group, x_ref, idx_ref, wr_ref, out_ref):
     groups, toks = out_ref.shape[1], x_ref.shape[0]
-    logits = nn_dot(x_ref[...], wr_ref[...]).T
+    logits = nt_dot(wr_ref[...], x_ref[...])
     expert = lax.broadcasted_iota(jnp.int32, logits.shape, 0)
     chosen = expert == idx_ref[0:1, :]
     for k in range(1, idx_ref.shape[0]):
@@ -262,10 +262,11 @@
     return jnp.where(column, v.astype(F32), 0.0).astype(BF16)
 
 
-def pass1_kernel(per_group, hot_ref, ep_ref, w1_ref, w3_ref, w2_ref, x_ref, d_ref, g_ref, xo_ref, do_ref, go_ref, ms_ref, *refs):
+def pass1_kernel(per_group, hot_ref, ep_ref, w1_ref, w3_ref, w2_ref, x_ref, d_ref, g_ref, xo_hbm, do_hbm, go_hbm, ms_ref, *refs):
     n_pair = g_ref.shape[0]
     n_sh, n_all = 2 * n_pair, hot_ref.shape[0]
-    gx_refs, (q_ref, act_ref, dz_ref, acto_ref, dzo_ref, r_scr) = refs[:n_sh], refs[n_sh:]
+    gx_hbms, (q_ref, act_ref, dz_ref, acto_ref, dzo_ref, r_scr, gx_scr, xo_ref, do_ref, go_ref, gx_sem, more_sem) = refs[:n_sh], refs[n_sh:]
+    more = [pltpu.make_async_copy(src, dst, more_sem.at[i]) for i, (src, dst) in enumerate(((xo_hbm, xo_ref), (do_hbm, do_ref), (go_hbm, go_ref)))]
     e = pl.program_id(0)
     ff = w1_ref.shape[2]
     w1, w3, w2 = w1_ref[0], w3_ref[0], w2_ref[0]
@@ -278,6 +279,8 @@
 
     @pl.when(e == 0)
     def _():
+        for c in more:
+            c.start()
         r_scr[:, base:, :] = jnp.zeros((n_sh, TAIL, r_scr.shape[2]), BF16)
         for i in range(per_group):
             r_scr[:, i * SPAN + SPAN - 16 : (i + 1) * SPAN, :] = jnp.zeros((n_sh, 16, r_scr.shape[2]), BF16)
@@ -295,6 +298,11 @@
         mask = slot_mask(m_of(j)[pl.ds(e, 1), :], SLOTS, 0)
         q_ref[pl.ds(j * per_group + e, 1), :] = jnp.sum(jnp.where(mask, q[rows], 0.0), axis=0, keepdims=True)
         r_scr[j, pl.ds(pl.multiple_of(e * SPAN, SPAN), SLOTS), :] = r[rows].astype(BF16)
+
+    @pl.when(e == 0)
+    def _():
+        for c in more:
+            c.wait()
 
     for first in range(0, n_all, n_sh):
         is_hot = [hot_ref[first + j, e] for j in range(n_sh)]
@@ -322,22 +330,41 @@
 
     @pl.when(e == per_group - 1)
     def _():
+        outs = []
         for j in range(n_sh):
             rank = m_of(j)[...]
             low = jnp.where(rank < SLOTS, rank, -1.0)
             masks = [slot_mask(low[i : i + 1, :], SPAN, 0) for i in range(per_group)]
             masks.append(slot_mask(extra_rank(rank), TAIL, SLOTS))
             pick = jnp.concatenate([m.astype(F32) for m in masks], axis=0).astype(BF16)
-            gx_refs[j][...] = tn_dot(pick, r_scr[j])
-
-
-def pass2_kernel(hot_ref, act_ref, dz_ref, x_ref, d_ref, xo_ref, do_ref, acto_ref, dzo_ref, g1_ref, g3_ref, g2_ref):
+            gx_scr[j] = tn_dot(pick, r_scr[j])
+            outs.append(pltpu.make_async_copy(gx_scr.at[j], gx_hbms[j], gx_sem.at[j]))
+            outs[j].start()
+        for c in outs:
+            c.wait()
+
+
+def pass2_kernel(hot_ref, act_ref, dz_ref, x_ref, d_ref, xo_hbm, do_hbm, acto_hbm, dzo_hbm, g1_ref, g3_ref, g2_ref, xo_ref, do_ref, acto_ref, dzo_ref, more_sem):
     e = pl.program_id(0)
+    pieces = ((xo_hbm, xo_ref), (do_hbm, do_ref), (acto_hbm, acto_ref), (dzo_hbm, dzo_ref))
+    more = [pltpu.make_async_copy(src, dst, more_sem.at[i]) for i, (src, dst) in enumerate(pieces)]
+
+    @pl.when(e == 0)
+    def _():
+        for c in more:
+            c.start()
+
     ff = g1_ref.shape[2]
     x = flat(x_ref)
     g1_ref[0] = tn_dot(x, dz_ref[0, :, :ff])
     g3_ref[0] = tn_dot(x, dz_ref[0, :, ff:])
     g2_ref[0] = tn_dot(act_ref[0], flat(d_ref))
+
+    @pl.when(e == 0)
+    def _():
+        for c in more:
+            c.wait()
+
     is_hot = [hot_ref[j, e] for j in range(hot_ref.shape[0])]
 
     @pl.when(sum(is_hot) > 0)
@@ -350,26 +377,35 @@
         g2_ref[0] += tn_dot(flat(acto_ref), masked(column, flat(do_ref)))
 
 
-def finish_kernel(per_group, ep_ref, own_ref, near_ref, far_ref, wr_ref, x0_ref, xs_ref, ms_ref, q_ref, gx_ref, gr_ref, acc):
-    n_sh, groups = q_ref.shape[0], wr_ref.shape[0]
+def finish_kernel(per_group, groups, ep_ref, own_ref, near_ref, far_ref, wr_ref, x0_ref, xs_ref, ms_ref, q_ref, gx_ref, gr_ref, wr_scr, acc):
+    n_sh = q_ref.shape[0]
     ep = ep_ref[0]
+    span = lambda m: slice(m * per_group, (m + 1) * per_group)
+    for a in range(groups):
+
+        @pl.when(ep == a)
+        def _():
+            for m in range(groups):
+                wr_scr[span(m), :] = wr_ref[span(a ^ m), :]
+
     for s in range(n_sh):
         d, j = divmod(s, groups)
-        rows = lambda m: slice((m ^ j) * per_group, ((m ^ j) + 1) * per_group)
-        q = [q_ref[d * groups + m, rows(m), :] for m in range(groups)]
+        q = [q_ref[d * groups + m, span(m ^ j), :] for m in range(groups)]
         p = [ms_ref[s, 0, ep ^ m][:per_group] for m in range(groups)]
         mean = sum(jnp.sum(a * b, axis=0, keepdims=True) for a, b in zip(p, q))
-        gap = jnp.zeros((PAD - per_group, q[0].shape[1]), F32)
-        dl = jnp.concatenate([v for a, b in zip(p, q) for v in (a * (b - mean), gap)], axis=0).astype(BF16)
+        dl = jnp.concatenate([a * (b - mean) for a, b in zip(p, q)], axis=0).astype(BF16)
         term = nn_dot(dl, x0_ref[...] if s == 0 else xs_ref[s - 1])
         if s == 0:
-            wr = jnp.concatenate([wr_ref[ep ^ m] for m in range(groups)], axis=0)
-            gx_ref[...] = (own_ref[...] + near_ref[...] + far_ref[...] + tn_dot(dl, wr)).astype(BF16)
+            gx_ref[...] = (own_ref[...] + near_ref[...] + far_ref[...] + tn_dot(dl, wr_scr[...])).astype(BF16)
             acc[...] = term
         else:
             acc[...] += term
-    for m in range(groups):
-        gr_ref[ep ^ m] = acc[m * PAD : (m + 1) * PAD, :]
+    for a in range(groups):
+
+        @pl.when(ep == a)
+        def _():
+            for m in range(groups):
+                gr_ref[span(a ^ m), :] = acc[span(m), :]
 
 
 def solution(mesh):
@@ -391,7 +427,6 @@
         vmem = pl.BlockSpec(memory_space=pltpu.VMEM)
         params = pltpu.CompilerParams(vmem_limit_bytes=VMEM_LIMIT)
 
-        wr_rows = jnp.pad(w_router.T.reshape(ep, n_loc, dim), ((0, 0), (0, PAD - n_loc), (0, 0)))
         m_shape = (2, ep, PAD, toks)
         hbm = pl.BlockSpec(memory_space=pl.ANY)
         main = n_loc * 2 * SLOTS
@@ -428,7 +463,7 @@
             compiler_params=pltpu.CompilerParams(collective_id=0, has_side_effects=True, vmem_limit_bytes=VMEM_LIMIT),
             cost_estimate=pl.CostEstimate(flops=2 * 10**10, bytes_accessed=5 * 10**7, transcendentals=0),
             name="near",
-        )(x_loc, dy_loc, route_idx.T, w_router)
+        )(x_loc, dy_loc, route_idx.T, w_router.T)
 
         w_specs = lambda im: [pl.BlockSpec((1, dim, ff), im), pl.BlockSpec((1, dim, ff), im), pl.BlockSpec((1, ff, dim), im)]
         im3 = lambda e, hot, ep_ref: (e, 0, 0)
@@ -451,20 +486,26 @@
                 in_specs=w_specs(im3)
                 + [pl.BlockSpec((pairs, 2 * SLOTS, dim), rows_at)] * 2
                 + [pl.BlockSpec((ep // 2, 2 * SLOTS, dim), rows_at)]
-                + [fix((pairs, 2 * EXTRA, dim))] * 2
-                + [fix((ep // 2, 2 * EXTRA, dim))]
+                + [hbm] * 3
                 + [pl.BlockSpec((ep, 1, 1, PAD, toks), lambda e, hot, ep_ref: (0, 0, ep_ref[0], 0, 0))],
-                out_specs=[fix((toks, dim))] * ep
+                out_specs=[hbm] * ep
                 + [fix((ep * n_loc, toks)), pl.BlockSpec((1, n_row, ff), im3), pl.BlockSpec((1, n_row, 2 * ff), im3)]
                 + [fix((pairs, 2 * EXTRA, ff)), fix((pairs, 2 * EXTRA, 2 * ff))],
-                scratch_shapes=[pltpu.VMEM((ep, n_loc * SPAN + TAIL, dim), BF16)],
+                scratch_shapes=[
+                    pltpu.VMEM((ep, n_loc * SPAN + TAIL, dim), BF16),
+                    pltpu.VMEM((ep, toks, dim), F32),
+                    pltpu.VMEM((pairs, 2 * EXTRA, dim), BF16),
+                    pltpu.VMEM((pairs, 2 * EXTRA, dim), BF16),
+                    pltpu.VMEM((ep // 2, 2 * EXTRA, dim), BF16),
+                    pltpu.SemaphoreType.DMA((ep,)),
+                    pltpu.SemaphoreType.DMA((3,)),
+                ],
             ),
             compiler_params=params,
             cost_estimate=pl.CostEstimate(flops=4 * 10**10, bytes_accessed=10**8, transcendentals=0),
             name="pass1",
         )(hot, ep_arr, w_gate, w_up, w_down, x_rows, d_rows, g_rows, x_more, d_more, g_more, ms)
 
-        from_core = swap(gx_part[1], 1)
         for_peer, q_all = pl.pallas_call(
             back_kernel,
             out_shape=[sds((toks, dim), F32), sds((n_dev, ep * n_loc, toks), F32)],
@@ -483,7 +524,9 @@
             cost_estimate=pl.CostEstimate(flops=8 * 10**9, bytes_accessed=5 * 10**7, transcendentals=0),
             name="back",
         )(q_loc, gx_part[2], gx_part[3])
+        for_peer, for_core = lax.optimization_barrier((for_peer, gx_part[1]))
         from_peer = swap(for_peer, 2)
+        from_core = swap(for_core, 1)
 
         im3 = lambda e, hot: (e, 0, 0)
         rows_at = lambda e, hot: (0, e, 0)
@@ -496,9 +539,15 @@
                 grid=(n_loc,),
                 in_specs=[pl.BlockSpec((1, n_row, ff), im3), pl.BlockSpec((1, n_row, 2 * ff), im3)]
                 + [pl.BlockSpec((pairs, 2 * SLOTS, dim), rows_at)] * 2
-                + [fix((pairs, 2 * EXTRA, dim))] * 2
-                + [fix((pairs, 2 * EXTRA, ff)), fix((pairs, 2 * EXTRA, 2 * ff))],
+                + [hbm] * 4,
                 out_specs=w_specs(im3),
+                scratch_shapes=[
+                    pltpu.VMEM((pairs, 2 * EXTRA, dim), BF16),
+                    pltpu.VMEM((pairs, 2 * EXTRA, dim), BF16),
+                    pltpu.VMEM((pairs, 2 * EXTRA, ff), BF16),
+                    pltpu.VMEM((pairs, 2 * EXTRA, 2 * ff), BF16),
+                    pltpu.SemaphoreType.DMA((4,)),
+                ],
             ),
             compiler_params=params,
             cost_estimate=pl.CostEstimate(flops=6 * 10**10, bytes_accessed=2 * 10**8, transcendentals=0),
@@ -507,21 +556,21 @@
 
         fixed = lambda shape: pl.BlockSpec(shape, lambda i, ep_ref: (0,) * len(shape))
         grad_x, grad_rt = pl.pallas_call(
-            functools.partial(finish_kernel, n_loc),
-            out_shape=[sds((toks, dim), BF16), sds((ep, PAD, dim), F32)],
+            functools.partial(finish_kernel, n_loc, ep),
+            out_shape=[sds((toks, dim), BF16), sds((n_exp, dim), F32)],
             grid_spec=pltpu.PrefetchScalarGridSpec(
                 num_scalar_prefetch=1,
                 grid=(1,),
-                in_specs=[fixed(v.shape) for v in (gx_part[0], from_core, from_peer, wr_rows, x_loc, xs)]
+                in_specs=[fixed(v.shape) for v in (gx_part[0], from_core, from_peer, w_router.T, x_loc, xs)]
                 + [pl.BlockSpec((n_dev, 1, ep, PAD, toks), lambda i, ep_ref: (0, 1, 0, 0, 0)), fixed(q_all.shape)],
-                out_specs=[fixed((toks, dim)), fixed((ep, PAD, dim))],
-                scratch_shapes=[pltpu.VMEM((ep * PAD, dim), F32)],
+                out_specs=[fixed((toks, dim)), fixed((n_exp, dim))],
+                scratch_shapes=[pltpu.VMEM((n_exp, dim), BF16), pltpu.VMEM((n_exp, dim), F32)],
             ),
             compiler_params=params,
             cost_estimate=pl.CostEstimate(flops=4 * 10**9, bytes_accessed=10**7, transcendentals=0),
             name="finish",
-        )(ep_arr, gx_part[0], from_core, from_peer, wr_rows, x_loc, xs, ms, q_all)
-        grad_router = grad_rt[:, :n_loc].reshape(n_exp, dim).T
+        )(ep_arr, gx_part[0], from_core, from_peer, w_router.T, x_loc, xs, ms, q_all)
+        grad_router = grad_rt.T
         return grad_x, grad_gate, grad_up, grad_down, grad_router
 
     return jax.shard_map(device_step, mesh=mesh, in_specs=(tok_spec, tok_spec, P(), exp_spec, exp_spec, exp_spec, tok_spec), out_specs=(tok_spec, exp_spec, exp_spec, exp_spec, P()), check_vma=False)

time: 208 us -> 198 us (0.952)
  Pallas kernels: 201 us -> 194 us
  local copies, waits for them, and re-layouts: 5.19 us -> 0 us
    pallas_call x1, Pallas kernels: 62.3 us -> 52.9 us  [device_step(): pl.pallas_call(functools.partial(pass1_kernel, n_loc), out_shape=[sds((to...]
    pallas_call x1, Pallas kernels: 9.46 us -> 16.8 us  [device_step(): pl.pallas_call(back_kernel, out_shape=[sds((toks, dim), F32), sds((n_dev,...]
    pallas_call x1, Pallas kernels: 54.7 us -> 50 us  [device_step(): pl.pallas_call(pass2_kernel, out_shape=[sds((n_loc, dim, ff), F32), sds((...]
    reshape x2 -> x0, local copies, waits for them, and re-layouts: 2.67 us -> none  [the longest x1 1.72 us: device_step(): grad_router = grad_rt[:, :n_loc].reshape(n_exp, dim).T]
  transfers between devices with their start and end apart: 2 -> 2, of which waited for: 0 -> 0; matrix products, arithmetic and copies ran while one was open for 1% -> 0% of each run, Pallas kernels for 31% -> 25%
where the time goes in v3:
time: 198 us; the launch traced here: 197 us
  Pallas kernels  194 us (98%)
    pallas_call x1, Pallas kernels, device_step(): pl.pallas_call(functools.partial(near_kernel, n_loc), out_shape=[sds((pai...  67.8 us
    pallas_call x1, Pallas kernels, device_step(): pl.pallas_call(functools.partial(pass1_kernel, n_loc), out_shape=[sds((to...  52.9 us
    pallas_call x1, Pallas kernels, device_step(): pl.pallas_call(pass2_kernel, out_shape=[sds((n_loc, dim, ff), F32), sds((...  50 us
    pallas_call x1, Pallas kernels, device_step(): pl.pallas_call(back_kernel, out_shape=[sds((toks, dim), F32), sds((n_dev,...  16.8 us
    pallas_call x1, Pallas kernels, device_step(): pl.pallas_call(functools.partial(finish_kernel, n_loc, ep), out_shape=[sd...  6.88 us
  transfers between devices with their start and end apart: 2, of which 0 were waited for; matrix products, arithmetic and copies ran while one was open for 0% of the time, Pallas kernels for 25%

profile of v3, /device:TPU:0, one launch (start us, length us, event | category | flops | bytes accessed | tf_op | source)
XLA Modules:
  0.0 196.9 jit_solution(17008553164375515824)
XLA Ops:
  0.6 67.8 %near.1 = (bf16[4,1120,1536]{2,1,0:T(8,128)(2,1)}, bf16[4,208,1536]{2,1,0:T(8,128)(2,1)}, bf16[4,1120,1536]{2,1,0:T(8,128)(2,1)}, bf16[4,208,1536]{2,1,0:T(8,128...) custom-call(bf16[256,1536]{1,0:T(8,128)(2,1)} %x0_ref.1, ...), custom_call_target="tpu_custom_call" | custom-call | flops 20000000000 | bytes 50000000 | tf_op jit(solution)/shard_map/near/pallas_call | solution.py:436
  68.4 52.9 %pass1.1 = (f32[256,1536]{1,0:T(8,128)}, f32[256,1536]{1,0:T(8,128)}, f32[256,1536]{1,0:T(8,128)}, f32[256,1536]{1,0:T(8,128)}, f32[40,256]{1,0:T(8,128)}, /*ind...) custom-call(s32[8,128]{1,0:T(8,128)} %get-tuple-element.32.hot_ref, ...), custom_call_target="tpu_custom_call" | custom-call | flops 40000000000 | bytes 100000000 | tf_op jit(solution)/shard_map/pass1/pallas_call | solution.py:473
  121.4 16.8 %back.1 = (f32[256,1536]{1,0:T(8,128)}, f32[8,40,256]{2,1,0:T(8,128)}) custom-call(f32[40,256]{1,0:T(8,128)} %get-tuple-element.41.q_ref, f32[256,1536]{1,0:T(8,128)} %get-tuple-element.42.keep_ref, f32[256,1536]{1,0:T(8,128)} %get-tuple-element.43.give_ref), custom_call_target="tpu_custom_call" | custom-call | flops 8000000000 | bytes 50000000 | tf_op jit(solution)/shard_map/back/pallas_call | solution.py:509
  138.2 0.4 collective-permute-start
  138.6 1.5 collective-permute-start.1
  140.1 50.0 %pass2.1 = (f32[10,1536,512]{2,1,0:T(8,128)}, f32[10,1536,512]{2,1,0:T(8,128)}, f32[10,512,1536]{2,1,0:T(8,128)}) custom-call(s32[8,128]{1,0:T(8,128)} %get-tuple-element.32.hot_ref, bf16[10,448,512]{2,1,0:T(8,128)(2,1)} %get-tuple-element.51.act_ref, bf16[10,448,1024]{2,1,0:T(8,128)(2,1)} %get-tuple-element.52.dz_ref, ...), custom_call_target="tpu_custom_call" | custom-call | flops 60000002048 | bytes 200000000 | tf_op jit(solution)/shard_map/pass2/pallas_call | solution.py:534
  190.0 0.0 collective-permute-done.near_ref
  190.1 0.0 collective-permute-done.1.far_ref
  190.1 6.9 %finish.1 = (bf16[256,1536]{1,0:T(8,128)(2,1)}, f32[40,1536]{1,0:T(8,128)}) custom-call(s32[1]{0:T(128)} %bitcast.ep_ref, f32[256,1536]{1,0:T(8,128)} %get-tuple-element.40.own_ref, f32[256,1536]{1,0:T(8,128)} %collective-permute-done.near_ref, f32[256,1536]{1,0:T(8,128)} %collective-permute-done.1.far_ref, bf16[40,1536]{1,0:T(8,128)(2,1)} %bitcast.5, ...), custom_call_target="tpu_custom_call" | custom-call | flops 4000000000 | bytes 10000000 | tf_op jit(solution)/shard_map/finish/pallas_call | solution.py:558
Async XLA Ops:
  138.2 51.8 %collective-permute-start = (f32[256,1536]{1,0:T(8,128)}, f32[256,1536]{1,0:T(8,128)}, u32[]{:S(2)}, u32[]{:S(2)}) collective-permute-start(f32[256,1536]{1,0:T(8,128)} %get-tuple-element.46), channel_id=1, source_target_pairs={{0,1},{1,0},{2,3},{3,2},{4,5},{5,4},{6,7},{7,6}} | collective-permute-start | bytes 4718600 | tf_op jit(solution)/shard_map/ppermute | solution.py:418
  138.6 51.5 %collective-permute-start.1 = (f32[256,1536]{1,0:T(8,128)}, f32[256,1536]{1,0:T(8,128)}, u32[]{:S(2)}, u32[]{:S(2)}) collective-permute-start(f32[256,1536]{1,0:T(8,128)} %get-tuple-element.47), channel_id=1, source_target_pairs={{0,2},{1,3},{2,0},{3,1},{4,6},{5,7},{6,4},{7,5}} | collective-permute-start | bytes 4718600 | tf_op jit(solution)/shard_map/ppermute | solution.py:418

commit v4 on v3

--- a/solution.py
+++ b/solution.py
@@ -101,15 +101,16 @@
     def __init__(self, main, bufs, sems, outs):
         self.main, self.bufs, self.sems, self.outs, self.busy, self.turn = main, bufs, sems, outs, {}, 0
 
-    def gather(self, i, kinds, *args):
+    def gather(self, index, *args):
+        kinds = len(index)
         slot, self.turn = self.turn, 1 - self.turn
         self.drain(slot)
         views = [self.bufs[k].at[slot] for k in range(kinds)]
         gather_rows(*args, *(views + [None])[:3])
         copies = []
         for k in range(kinds):
-            copies.append(pltpu.make_async_copy(views[k].at[pl.ds(0, self.main)], self.outs[2 * k].at[i], self.sems.at[slot, 2 * k]))
-            copies.append(pltpu.make_async_copy(views[k].at[pl.ds(self.main, 2 * EXTRA)], self.outs[2 * k + 1].at[i], self.sems.at[slot, 2 * k + 1]))
+            copies.append(pltpu.make_async_copy(views[k].at[pl.ds(0, self.main)], self.outs[2 * k].at[index[k]], self.sems.at[slot, 2 * k]))
+            copies.append(pltpu.make_async_copy(views[k].at[pl.ds(self.main, 2 * EXTRA)], self.outs[2 * k + 1].at[index[k]], self.sems.at[slot, 2 * k + 1]))
         for c in copies:
             c.start()
         self.busy[slot] = copies
@@ -130,10 +131,18 @@
     pl.semaphore_wait(barrier, len(bits))
 
 
-def near_kernel(per_group, x_ref, g_ref, idx_ref, wr_ref, *refs):
-    rows_out, (xs_out, ms_out, hot_out) = refs[:6], refs[6:9]
-    x_in, g_in, i_in, st_x, st_d, st_g, send, recv, out_sem, st_sem = refs[9:]
+def near_kernel(per_group, x_ref, g_ref, idx_ref, wr_ref, w1_hbm, w3_hbm, w2_hbm, *refs):
+    rows_out, (xs_out, act_out, dz_out, ms_out, hot_out, q_out) = refs[:6], refs[6:12]
+    x_in, g_in, i_in, st_x, st_d, st_g, w1_buf, w3_buf, w2_buf, act_scr, dz_scr, send, recv, out_sem, st_sem, w_sem = refs[12:]
     me = lax.axis_index("ep")
+    n_dev = hot_out.shape[0]
+
+    def weights(e, slot):
+        pairs = ((w1_hbm, w1_buf), (w3_hbm, w3_buf), (w2_hbm, w2_buf))
+        return [pltpu.make_async_copy(src.at[e], dst.at[slot], w_sem.at[slot, i]) for i, (src, dst) in enumerate(pairs)]
+
+    for c in weights(0, 0):
+        c.start()
     greet((1, 2, 4))
     own = (x_ref, g_ref, idx_ref)
     land = lambda s: own if s == 0 else (x_in.at[s - 1], g_in.at[s - 1], i_in.at[s - 1])
@@ -163,11 +172,37 @@
         hot = hot_rows(ms_out[s, 0, me]).astype(jnp.int32)
         shape = (hot.shape[0], hot_out.shape[1])
         diagonal = lax.broadcasted_iota(jnp.int32, shape, 0) == lax.broadcasted_iota(jnp.int32, shape, 1)
-        hot_out[s : s + 1, :] = jnp.sum(jnp.where(diagonal, hot, 0), axis=0, keepdims=True)
+        row = (s - 2) % n_dev
+        hot_out[row : row + 1, :] = jnp.sum(jnp.where(diagonal, hot, 0), axis=0, keepdims=True)
 
     def gather(s):
         pair = (s, s + 1)
-        stage.gather(s // 2, 3 if s < 4 else 2, me, per_group, [ms_out.at[i] for i in pair], [land(i)[0] for i in pair], [land(i)[1] for i in pair])
+        place = (s // 2 - 1) % (n_dev // 2)
+        index = (place, place, 1 - s // 2) if s < 4 else (place, place)
+        stage.gather(index, me, per_group, [ms_out.at[i] for i in pair], [land(i)[0] for i in pair], [land(i)[1] for i in pair])
+
+    def own_chip(e, carry):
+        slot = lax.rem(e, 2)
+        for c in weights(e, slot):
+            c.wait()
+
+        @pl.when(e + 1 < per_group)
+        def _():
+            for c in weights(e + 1, 1 - slot):
+                c.start()
+
+        ff = act_scr.shape[2]
+        rows = pl.ds(pl.multiple_of(e * (2 * SLOTS), 16), 2 * SLOTS)
+        w2 = w2_buf[slot]
+        act, dz1, dz3 = expert_math(st_x[0, rows, :], st_d[0, rows, :], w1_buf[slot], w3_buf[slot], w2)
+        act_scr[e] = act
+        dz_scr[e, :, :ff] = dz1
+        dz_scr[e, :, ff:] = dz3
+        q = jnp.sum(nn_dot(act, w2) * st_g[0, rows, :].astype(F32), axis=1, keepdims=True)
+        for j in range(2):
+            mask = slot_mask(ms_out[j, 0, me, pl.ds(e, 1), :], SLOTS, 0)
+            q_out[pl.ds(j * per_group + e, 1), :] = jnp.sum(jnp.where(mask, q[j * SLOTS : (j + 1) * SLOTS], 0.0), axis=0, keepdims=True)
+        return carry
 
     X, G, I = range(3)
     for k in (X, I, G):
@@ -181,6 +216,11 @@
         arrive(k, 1)
     routing(1)
     gather(0)
+    lax.fori_loop(0, per_group, own_chip, 0)
+    for i, (src, dst) in enumerate(((act_scr, act_out), (dz_scr, dz_out))):
+        c = pltpu.make_async_copy(src, dst, out_sem.at[n_dev - 1 + i])
+        c.start()
+        outs.append(c)
     arrive(X, 2, (6, 4), (3, 1))
     arrive(I, 2, (6, 4), (3, 1))
     arrive(G, 4, (6, 2), (5, 1))
@@ -262,20 +302,22 @@
     return jnp.where(column, v.astype(F32), 0.0).astype(BF16)
 
 
-def pass1_kernel(per_group, hot_ref, ep_ref, w1_ref, w3_ref, w2_ref, x_ref, d_ref, g_ref, xo_hbm, do_hbm, go_hbm, ms_ref, *refs):
-    n_pair = g_ref.shape[0]
-    n_sh, n_all = 2 * n_pair, hot_ref.shape[0]
+def pass1_kernel(per_group, order, hot_ref, ep_ref, w1_ref, w3_ref, w2_ref, x_ref, d_ref, g_ref, dz01_ref, q01_ref, xo_hbm, do_hbm, go_hbm, ms_ref, *refs):
+    n_sh, n_all = len(order), hot_ref.shape[0]
     gx_hbms, (q_ref, act_ref, dz_ref, acto_ref, dzo_ref, r_scr, gx_scr, xo_ref, do_ref, go_ref, gx_sem, more_sem) = refs[:n_sh], refs[n_sh:]
     more = [pltpu.make_async_copy(src, dst, more_sem.at[i]) for i, (src, dst) in enumerate(((xo_hbm, xo_ref), (do_hbm, do_ref), (go_hbm, go_ref)))]
     e = pl.program_id(0)
     ff = w1_ref.shape[2]
     w1, w3, w2 = w1_ref[0], w3_ref[0], w2_ref[0]
     base = per_group * SPAN
-    m_of = lambda j: ms_ref.at[j, 0, 0]
-
-    def token_math(act, dz1, dz3, g):
-        q = jnp.sum(nn_dot(act, w2) * g.astype(F32), axis=1, keepdims=True)
-        return q, nt_dot(dz1, w1) + nt_dot(dz3, w3)
+    m_of = lambda i: ms_ref.at[order[i], 0, 0]
+    q_row = lambda i: pl.ds(order[i] * per_group + e, 1)
+
+    def q_math(act, g):
+        return jnp.sum(nn_dot(act, w2) * g.astype(F32), axis=1, keepdims=True)
+
+    def r_math(dz1, dz3):
+        return nt_dot(dz1, w1) + nt_dot(dz3, w3)
 
     @pl.when(e == 0)
     def _():
@@ -286,65 +328,71 @@
             r_scr[:, i * SPAN + SPAN - 16 : (i + 1) * SPAN, :] = jnp.zeros((n_sh, 16, r_scr.shape[2]), BF16)
         acto_ref[...] = jnp.zeros_like(acto_ref)
         dzo_ref[...] = jnp.zeros_like(dzo_ref)
+        q_ref[: 2 * per_group, :] = q01_ref[...]
 
     act, dz1, dz3 = expert_math(flat(x_ref), flat(d_ref), w1, w3, w2)
     act_ref[0] = act
     dz_ref[0, :, :ff] = dz1
     dz_ref[0, :, ff:] = dz3
-    near = n_sh * SLOTS
-    q, r = token_math(act[:near], dz1[:near], dz3[:near], flat(g_ref))
-    for j in range(n_sh):
-        rows = slice(j * SLOTS, (j + 1) * SLOTS)
-        mask = slot_mask(m_of(j)[pl.ds(e, 1), :], SLOTS, 0)
-        q_ref[pl.ds(j * per_group + e, 1), :] = jnp.sum(jnp.where(mask, q[rows], 0.0), axis=0, keepdims=True)
-        r_scr[j, pl.ds(pl.multiple_of(e * SPAN, SPAN), SLOTS), :] = r[rows].astype(BF16)
+    near = 2 * SLOTS
+    q = q_math(act[:near], flat(g_ref))
+    r = r_math(jnp.concatenate([dz1[:near], dz01_ref[0, :, :ff]], axis=0), jnp.concatenate([dz3[:near], dz01_ref[0, :, ff:]], axis=0))
+    for i in range(n_sh):
+        rows = slice(i * SLOTS, (i + 1) * SLOTS)
+        if i < 2:
+            mask = slot_mask(m_of(i)[pl.ds(e, 1), :], SLOTS, 0)
+            q_ref[q_row(i), :] = jnp.sum(jnp.where(mask, q[rows], 0.0), axis=0, keepdims=True)
+        r_scr[i, pl.ds(pl.multiple_of(e * SPAN, SPAN), SLOTS), :] = r[rows].astype(BF16)
 
     @pl.when(e == 0)
     def _():
         for c in more:
             c.wait()
 
-    for first in range(0, n_all, n_sh):
-        is_hot = [hot_ref[first + j, e] for j in range(n_sh)]
+    last = n_all // 2 - 1
+    for near_part in (True, False):
+        places = (0, last) if near_part else tuple(range(1, last))
+        is_hot = [hot_ref[2 * place + k, e] for place in places for k in range(2)]
 
         @pl.when(sum(is_hot) > 0)
         def _():
-            part = first // 2
             column = hot_column(is_hot)
-            d = masked(column, flat(do_ref, part, n_pair))
-            act, dz1, dz3 = expert_math(flat(xo_ref, part, n_pair), d, w1, w3, w2)
-            shape = (n_pair, 2 * EXTRA, ff)
-            acto_ref[part : part + n_pair] += masked(column, act).reshape(shape)
-            dzo_ref[part : part + n_pair, :, :ff] += dz1.reshape(shape)
-            dzo_ref[part : part + n_pair, :, ff:] += dz3.reshape(shape)
-            if first == 0:
-                q, r = token_math(act, dz1, dz3, flat(go_ref))
-                for j in range(n_sh):
-                    rows = slice(j * EXTRA, (j + 1) * EXTRA)
-
-                    @pl.when(is_hot[j] > 0)
+            take = lambda ref: jnp.concatenate([ref[place] for place in places], axis=0)
+            act, dz1, dz3 = expert_math(take(xo_ref), masked(column, take(do_ref)), w1, w3, w2)
+            kept = masked(column, act)
+            for i, place in enumerate(places):
+                rows = slice(i * 2 * EXTRA, (i + 1) * 2 * EXTRA)
+                acto_ref[place] += kept[rows]
+                dzo_ref[place, :, :ff] += dz1[rows]
+                dzo_ref[place, :, ff:] += dz3[rows]
+            if near_part:
+                q, r = q_math(act, flat(go_ref)), r_math(dz1, dz3)
+                for i in range(n_sh):
+                    rows = slice(i * EXTRA, (i + 1) * EXTRA)
+
+                    @pl.when(is_hot[i] > 0)
                     def _():
-                        mask = slot_mask(m_of(j)[pl.ds(e, 1), :], EXTRA, SLOTS)
-                        q_ref[pl.ds(j * per_group + e, 1), :] += jnp.sum(jnp.where(mask, q[rows], 0.0), axis=0, keepdims=True)
-                        r_scr[j, base : base + EXTRA, :] = r[rows].astype(BF16)
+                        mask = slot_mask(m_of(i)[pl.ds(e, 1), :], EXTRA, SLOTS)
+                        q_ref[q_row(i), :] += jnp.sum(jnp.where(mask, q[rows], 0.0), axis=0, keepdims=True)
+                        r_scr[i, base : base + EXTRA, :] = r[rows].astype(BF16)
 
     @pl.when(e == per_group - 1)
     def _():
         outs = []
-        for j in range(n_sh):
-            rank = m_of(j)[...]
+        for i in range(n_sh - 1, -1, -1):
+            rank = m_of(i)[...]
             low = jnp.where(rank < SLOTS, rank, -1.0)
-            masks = [slot_mask(low[i : i + 1, :], SPAN, 0) for i in range(per_group)]
+            masks = [slot_mask(low[k : k + 1, :], SPAN, 0) for k in range(per_group)]
             masks.append(slot_mask(extra_rank(rank), TAIL, SLOTS))
             pick = jnp.concatenate([m.astype(F32) for m in masks], axis=0).astype(BF16)
-            gx_scr[j] = tn_dot(pick, r_scr[j])
-            outs.append(pltpu.make_async_copy(gx_scr.at[j], gx_hbms[j], gx_sem.at[j]))
-            outs[j].start()
+            gx_scr[i] = tn_dot(pick, r_scr[i])
+            outs.append(pltpu.make_async_copy(gx_scr.at[i], gx_hbms[order[i]], gx_sem.at[i]))
+            outs[-1].start()
         for c in outs:
             c.wait()
 
 
-def pass2_kernel(hot_ref, act_ref, dz_ref, x_ref, d_ref, xo_hbm, do_hbm, acto_hbm, dzo_hbm, g1_ref, g3_ref, g2_ref, xo_ref, do_ref, acto_ref, dzo_ref, more_sem):
+def pass2_kernel(hot_ref, act_ref, dz_ref, act01_ref, dz01_ref, x_ref, d_ref, xo_hbm, do_hbm, acto_hbm, dzo_hbm, g1_ref, g3_ref, g2_ref, xo_ref, do_ref, acto_ref, dzo_ref, more_sem):
     e = pl.program_id(0)
     pieces = ((xo_hbm, xo_ref), (do_hbm, do_ref), (acto_hbm, acto_ref), (dzo_hbm, dzo_ref))
     more = [pltpu.make_async_copy(src, dst, more_sem.at[i]) for i, (src, dst) in enumerate(pieces)]
@@ -356,9 +404,9 @@
 
     ff = g1_ref.shape[2]
     x = flat(x_ref)
-    g1_ref[0] = tn_dot(x, dz_ref[0, :, :ff])
-    g3_ref[0] = tn_dot(x, dz_ref[0, :, ff:])
-    g2_ref[0] = tn_dot(act_ref[0], flat(d_ref))
+    g1_ref[0] = tn_dot(x, jnp.concatenate([dz_ref[0, :, :ff], dz01_ref[0, :, :ff]], axis=0))
+    g3_ref[0] = tn_dot(x, jnp.concatenate([dz_ref[0, :, ff:], dz01_ref[0, :, ff:]], axis=0))
+    g2_ref[0] = tn_dot(jnp.concatenate([act_ref[0], act01_ref[0]], axis=0), flat(d_ref))
 
     @pl.when(e == 0)
     def _():
@@ -433,7 +481,7 @@
         pairs = n_dev // 2
         sds = jax.ShapeDtypeStruct
         others = n_dev - 1
-        x_rows, x_more, d_rows, d_more, g_rows, g_more, xs, ms, hot = pl.pallas_call(
+        x_rows, x_more, d_rows, d_more, g_rows, g_more, xs, act01, dz01, ms, hot, q01 = pl.pallas_call(
             functools.partial(near_kernel, n_loc),
             out_shape=[
                 sds((pairs, main, dim), BF16),
@@ -443,11 +491,14 @@
                 sds((ep // 2, main, dim), BF16),
                 sds((ep // 2, 2 * EXTRA, dim), BF16),
                 sds((others, toks, dim), BF16),
+                sds((n_loc, 2 * SLOTS, ff), BF16),
+                sds((n_loc, 2 * SLOTS, 2 * ff), BF16),
                 sds((n_dev,) + m_shape, F32),
                 sds((n_dev, 128), jnp.int32),
+                sds((2 * n_loc, toks), F32),
             ],
-            in_specs=[vmem] * 4,
-            out_specs=[hbm] * 7 + [vmem] * 2,
+            in_specs=[vmem] * 4 + [hbm] * 3,
+            out_specs=[hbm] * 9 + [vmem] * 3,
             scratch_shapes=[
                 pltpu.VMEM((others, toks, dim), BF16),
                 pltpu.VMEM((others, toks, dim), BF16),
@@ -455,23 +506,29 @@
                 pltpu.VMEM((2, main + 2 * EXTRA, dim), BF16),
                 pltpu.VMEM((2, main + 2 * EXTRA, dim), BF16),
                 pltpu.VMEM((2, main + 2 * EXTRA, dim), BF16),
+                pltpu.VMEM((2, dim, ff), BF16),
+                pltpu.VMEM((2, dim, ff), BF16),
+                pltpu.VMEM((2, ff, dim), BF16),
+                pltpu.VMEM((n_loc, 2 * SLOTS, ff), BF16),
+                pltpu.VMEM((n_loc, 2 * SLOTS, 2 * ff), BF16),
                 pltpu.SemaphoreType.DMA((others, 3)),
                 pltpu.SemaphoreType.DMA((others, 3)),
-                pltpu.SemaphoreType.DMA((others,)),
+                pltpu.SemaphoreType.DMA((others + 2,)),
                 pltpu.SemaphoreType.DMA((2, 6)),
+                pltpu.SemaphoreType.DMA((2, 3)),
             ],
             compiler_params=pltpu.CompilerParams(collective_id=0, has_side_effects=True, vmem_limit_bytes=VMEM_LIMIT),
             cost_estimate=pl.CostEstimate(flops=2 * 10**10, bytes_accessed=5 * 10**7, transcendentals=0),
             name="near",
-        )(x_loc, dy_loc, route_idx.T, w_router.T)
+        )(x_loc, dy_loc, route_idx.T, w_router.T, w_gate, w_up, w_down)
 
         w_specs = lambda im: [pl.BlockSpec((1, dim, ff), im), pl.BlockSpec((1, dim, ff), im), pl.BlockSpec((1, ff, dim), im)]
         im3 = lambda e, hot, ep_ref: (e, 0, 0)
         rows_at = lambda e, hot, ep_ref: (0, e, 0)
         fix = lambda shape: pl.BlockSpec(shape, lambda e, hot, ep_ref: (0,) * len(shape), pipeline_mode=pl.Buffered(1))
-        n_row = n_dev * SLOTS
+        n_row = (n_dev - 2) * SLOTS
         *gx_part, q_loc, act, dz, act_more, dz_more = pl.pallas_call(
-            functools.partial(pass1_kernel, n_loc),
+            functools.partial(pass1_kernel, n_loc, (2, 3, 0, 1)),
             out_shape=[sds((toks, dim), F32)] * ep
             + [
                 sds((ep * n_loc, toks), F32),
@@ -484,8 +541,8 @@
                 num_scalar_prefetch=2,
                 grid=(n_loc,),
                 in_specs=w_specs(im3)
-                + [pl.BlockSpec((pairs, 2 * SLOTS, dim), rows_at)] * 2
-                + [pl.BlockSpec((ep // 2, 2 * SLOTS, dim), rows_at)]
+                + [pl.BlockSpec((pairs - 1, 2 * SLOTS, dim), rows_at)] * 2
+                + [pl.BlockSpec((1, 2 * SLOTS, dim), rows_at), pl.BlockSpec((1, 2 * SLOTS, 2 * ff), im3), fix((2 * n_loc, toks))]
                 + [hbm] * 3
                 + [pl.BlockSpec((ep, 1, 1, PAD, toks), lambda e, hot, ep_ref: (0, 0, ep_ref[0], 0, 0))],
                 out_specs=[hbm] * ep
@@ -504,7 +561,7 @@
             compiler_params=params,
             cost_estimate=pl.CostEstimate(flops=4 * 10**10, bytes_accessed=10**8, transcendentals=0),
             name="pass1",
-        )(hot, ep_arr, w_gate, w_up, w_down, x_rows, d_rows, g_rows, x_more, d_more, g_more, ms)
+        )(hot, ep_arr, w_gate, w_up, w_down, x_rows, d_rows, g_rows, dz01, q01, x_more, d_more, g_more, ms)
 
         for_peer, q_all = pl.pallas_call(
             back_kernel,
@@ -538,6 +595,7 @@
                 num_scalar_prefetch=1,
                 grid=(n_loc,),
                 in_specs=[pl.BlockSpec((1, n_row, ff), im3), pl.BlockSpec((1, n_row, 2 * ff), im3)]
+                + [pl.BlockSpec((1, 2 * SLOTS, ff), im3), pl.BlockSpec((1, 2 * SLOTS, 2 * ff), im3)]
                 + [pl.BlockSpec((pairs, 2 * SLOTS, dim), rows_at)] * 2
                 + [hbm] * 4,
                 out_specs=w_specs(im3),
@@ -552,7 +610,7 @@
             compiler_params=params,
             cost_estimate=pl.CostEstimate(flops=6 * 10**10, bytes_accessed=2 * 10**8, transcendentals=0),
             name="pass2",
-        )(hot, act, dz, x_rows, d_rows, x_more, d_more, act_more, dz_more)
+        )(hot, act, dz, act01, dz01, x_rows, d_rows, x_more, d_more, act_more, dz_more)
 
         fixed = lambda shape: pl.BlockSpec(shape, lambda i, ep_ref: (0,) * len(shape))
         grad_x, grad_rt = pl.pallas_call(

time: 198 us -> 193 us (0.975)
  Pallas kernels: 194 us -> 188 us
    pallas_call x1, Pallas kernels: 52.9 us -> 46.2 us  [device_step(): pl.pallas_call(functools.partial(pass1_kernel, n_loc, (2, 3, 0, 1)), out_...]
  transfers between devices with their start and end apart: 2 -> 2, of which waited for: 0 -> 0; matrix products, arithmetic and copies ran while one was open for 0% -> 0% of each run, Pallas kernels for 25% -> 26%
where the time goes in v4:
time: 193 us; the launch traced here: 190 us
  Pallas kernels  188 us (97%)
    pallas_call x1, Pallas kernels, device_step(): pl.pallas_call(functools.partial(near_kernel, n_loc), out_shape=[sds((pai...  69.2 us
    pallas_call x1, Pallas kernels, device_step(): pl.pallas_call(pass2_kernel, out_shape=[sds((n_loc, dim, ff), F32), sds((...  50.2 us
    pallas_call x1, Pallas kernels, device_step(): pl.pallas_call(functools.partial(pass1_kernel, n_loc, (2, 3, 0, 1)), out_...  46.2 us
    pallas_call x1, Pallas kernels, device_step(): pl.pallas_call(back_kernel, out_shape=[sds((toks, dim), F32), sds((n_dev,...  15.9 us
    pallas_call x1, Pallas kernels, device_step(): pl.pallas_call(functools.partial(finish_kernel, n_loc, ep), out_shape=[sd...  6.88 us
  transfers between devices with their start and end apart: 2, of which 0 were waited for; matrix products, arithmetic and copies ran while one was open for 0% of the time, Pallas kernels for 26%

profile of v4, /device:TPU:0, one launch (start us, length us, event | category | flops | bytes accessed | tf_op | source)
XLA Modules:
  0.0 190.0 jit_solution(14655824525092343525)
XLA Ops:
  0.6 69.2 %near.1 = (bf16[4,1120,1536]{2,1,0:T(8,128)(2,1)}, bf16[4,208,1536]{2,1,0:T(8,128)(2,1)}, bf16[4,1120,1536]{2,1,0:T(8,128)(2,1)}, bf16[4,208,1536]{2,1,0:T(8,128...) custom-call(bf16[256,1536]{1,0:T(8,128)(2,1)} %x0_ref.1, ...), custom_call_target="tpu_custom_call" | custom-call | flops 20000000000 | bytes 50000000 | tf_op jit(solution)/shard_map/near/pallas_call | solution.py:484
  69.9 46.2 %pass1.1 = (f32[256,1536]{1,0:T(8,128)}, f32[256,1536]{1,0:T(8,128)}, f32[256,1536]{1,0:T(8,128)}, f32[256,1536]{1,0:T(8,128)}, f32[40,256]{1,0:T(8,128)}, /*ind...) custom-call(s32[8,128]{1,0:T(8,128)} %get-tuple-element.35.hot_ref, ...), custom_call_target="tpu_custom_call" | custom-call | flops 40000000000 | bytes 100000000 | tf_op jit(solution)/shard_map/pass1/pallas_call | solution.py:530
  116.0 15.9 %back.1 = (f32[256,1536]{1,0:T(8,128)}, f32[8,40,256]{2,1,0:T(8,128)}) custom-call(f32[40,256]{1,0:T(8,128)} %get-tuple-element.46.q_ref, f32[256,1536]{1,0:T(8,128)} %get-tuple-element.47.keep_ref, f32[256,1536]{1,0:T(8,128)} %get-tuple-element.48.give_ref), custom_call_target="tpu_custom_call" | custom-call | flops 8000000000 | bytes 50000000 | tf_op jit(solution)/shard_map/back/pallas_call | solution.py:566
  132.0 0.4 collective-permute-start
  132.4 0.6 collective-permute-start.1
  132.9 50.2 %pass2.1 = (f32[10,1536,512]{2,1,0:T(8,128)}, f32[10,1536,512]{2,1,0:T(8,128)}, f32[10,512,1536]{2,1,0:T(8,128)}) custom-call(s32[8,128]{1,0:T(8,128)} %get-tuple-element.35.hot_ref, bf16[10,336,512]{2,1,0:T(8,128)(2,1)} %get-tuple-element.56.act_ref, bf16[10,336,1024]{2,1,0:T(8,128)(2,1)} %get-tuple-element.57.dz_ref, ...), custom_call_target="tpu_custom_call" | custom-call | flops 60000002048 | bytes 200000000 | tf_op jit(solution)/shard_map/pass2/pallas_call | solution.py:591
  183.1 0.0 collective-permute-done.near_ref
  183.1 0.0 collective-permute-done.1.far_ref
  183.1 6.9 %finish.1 = (bf16[256,1536]{1,0:T(8,128)(2,1)}, f32[40,1536]{1,0:T(8,128)}) custom-call(s32[1]{0:T(128)} %bitcast.ep_ref, f32[256,1536]{1,0:T(8,128)} %get-tuple-element.45.own_ref, f32[256,1536]{1,0:T(8,128)} %collective-permute-done.near_ref, f32[256,1536]{1,0:T(8,128)} %collective-permute-done.1.far_ref, bf16[40,1536]{1,0:T(8,128)(2,1)} %bitcast.5, ...), custom_call_target="tpu_custom_call" | custom-call | flops 4000000000 | bytes 10000000 | tf_op jit(solution)/shard_map/finish/pallas_call | solution.py:616
Async XLA Ops:
  132.0 51.1 %collective-permute-start = (f32[256,1536]{1,0:T(8,128)}, f32[256,1536]{1,0:T(8,128)}, u32[]{:S(2)}, u32[]{:S(2)}) collective-permute-start(f32[256,1536]{1,0:T(8,128)} %get-tuple-element.51), channel_id=1, source_target_pairs={{0,1},{1,0},{2,3},{3,2},{4,5},{5,4},{6,7},{7,6}} | collective-permute-start | bytes 4718600 | tf_op jit(solution)/shard_map/ppermute | solution.py:466
  132.4 50.8 %collective-permute-start.1 = (f32[256,1536]{1,0:T(8,128)}, f32[256,1536]{1,0:T(8,128)}, u32[]{:S(2)}, u32[]{:S(2)}) collective-permute-start(f32[256,1536]{1,0:T(8,128)} %get-tuple-element.52), channel_id=1, source_target_pairs={{0,2},{1,3},{2,0},{3,1},{4,6},{5,7},{6,4},{7,5}} | collective-permute-start | bytes 4718600 | tf_op jit(solution)/shard_map/ppermute | solution.py:466

commit v5 on v4

--- a/solution.py
+++ b/solution.py
@@ -238,12 +238,14 @@
         arrive(k, 5)
     routing(5)
     gather(4)
-    for k in (X, I, G):
+    for k in (X, I):
         arrive(k, 6, (7, 1))
     routing(6)
-    for k in (X, I, G):
+    arrive(G, 6, (7, 1))
+    for k in (X, I):
         arrive(k, 7)
     routing(7)
+    arrive(G, 7)
     gather(6)
     stage.drain(0)
     stage.drain(1)
@@ -302,9 +304,9 @@
     return jnp.where(column, v.astype(F32), 0.0).astype(BF16)
 
 
-def pass1_kernel(per_group, order, hot_ref, ep_ref, w1_ref, w3_ref, w2_ref, x_ref, d_ref, g_ref, dz01_ref, q01_ref, xo_hbm, do_hbm, go_hbm, ms_ref, *refs):
+def pass1_kernel(per_group, order, hot_ref, ep_ref, w1_ref, w3_ref, w2_ref, x_ref, d_ref, g_ref, act01_ref, dz01_ref, q01_ref, xo_hbm, do_hbm, go_hbm, ms_ref, *refs):
     n_sh, n_all = len(order), hot_ref.shape[0]
-    gx_hbms, (q_ref, act_ref, dz_ref, acto_ref, dzo_ref, r_scr, gx_scr, xo_ref, do_ref, go_ref, gx_sem, more_sem) = refs[:n_sh], refs[n_sh:]
+    gx_hbms, (q_ref, g2_ref, dz_ref, dzo_ref, r_scr, gx_scr, xo_ref, do_ref, go_ref, gx_sem, more_sem) = refs[:n_sh], refs[n_sh:]
     more = [pltpu.make_async_copy(src, dst, more_sem.at[i]) for i, (src, dst) in enumerate(((xo_hbm, xo_ref), (do_hbm, do_ref), (go_hbm, go_ref)))]
     e = pl.program_id(0)
     ff = w1_ref.shape[2]
@@ -326,12 +328,12 @@
         r_scr[:, base:, :] = jnp.zeros((n_sh, TAIL, r_scr.shape[2]), BF16)
         for i in range(per_group):
             r_scr[:, i * SPAN + SPAN - 16 : (i + 1) * SPAN, :] = jnp.zeros((n_sh, 16, r_scr.shape[2]), BF16)
-        acto_ref[...] = jnp.zeros_like(acto_ref)
         dzo_ref[...] = jnp.zeros_like(dzo_ref)
         q_ref[: 2 * per_group, :] = q01_ref[...]
 
-    act, dz1, dz3 = expert_math(flat(x_ref), flat(d_ref), w1, w3, w2)
-    act_ref[0] = act
+    d = flat(d_ref)
+    act, dz1, dz3 = expert_math(flat(x_ref), d[: x_ref.shape[0] * x_ref.shape[1]], w1, w3, w2)
+    g2_ref[0] = tn_dot(jnp.concatenate([act, act01_ref[0]], axis=0), d)
     dz_ref[0, :, :ff] = dz1
     dz_ref[0, :, ff:] = dz3
     near = 2 * SLOTS
@@ -358,11 +360,11 @@
         def _():
             column = hot_column(is_hot)
             take = lambda ref: jnp.concatenate([ref[place] for place in places], axis=0)
-            act, dz1, dz3 = expert_math(take(xo_ref), masked(column, take(do_ref)), w1, w3, w2)
-            kept = masked(column, act)
+            d = masked(column, take(do_ref))
+            act, dz1, dz3 = expert_math(take(xo_ref), d, w1, w3, w2)
+            g2_ref[0] += tn_dot(act, d)
             for i, place in enumerate(places):
                 rows = slice(i * 2 * EXTRA, (i + 1) * 2 * EXTRA)
-                acto_ref[place] += kept[rows]
                 dzo_ref[place, :, :ff] += dz1[rows]
                 dzo_ref[place, :, ff:] += dz3[rows]
             if near_part:
@@ -392,9 +394,9 @@
             c.wait()
 
 
-def pass2_kernel(hot_ref, act_ref, dz_ref, act01_ref, dz01_ref, x_ref, d_ref, xo_hbm, do_hbm, acto_hbm, dzo_hbm, g1_ref, g3_ref, g2_ref, xo_ref, do_ref, acto_ref, dzo_ref, more_sem):
+def pass2_kernel(hot_ref, dz_ref, dz01_ref, x_ref, xo_hbm, dzo_hbm, g1_ref, g3_ref, xo_ref, dzo_ref, more_sem):
     e = pl.program_id(0)
-    pieces = ((xo_hbm, xo_ref), (do_hbm, do_ref), (acto_hbm, acto_ref), (dzo_hbm, dzo_ref))
+    pieces = ((xo_hbm, xo_ref), (dzo_hbm, dzo_ref))
     more = [pltpu.make_async_copy(src, dst, more_sem.at[i]) for i, (src, dst) in enumerate(pieces)]
 
     @pl.when(e == 0)
@@ -406,7 +408,6 @@
     x = flat(x_ref)
     g1_ref[0] = tn_dot(x, jnp.concatenate([dz_ref[0, :, :ff], dz01_ref[0, :, :ff]], axis=0))
     g3_ref[0] = tn_dot(x, jnp.concatenate([dz_ref[0, :, ff:], dz01_ref[0, :, ff:]], axis=0))
-    g2_ref[0] = tn_dot(jnp.concatenate([act_ref[0], act01_ref[0]], axis=0), flat(d_ref))
 
     @pl.when(e == 0)
     def _():
@@ -422,7 +423,6 @@
         dz = masked(column, flat(dzo_ref))
         g1_ref[0] += tn_dot(x, dz[:, :ff])
         g3_ref[0] += tn_dot(x, dz[:, ff:])
-        g2_ref[0] += tn_dot(flat(acto_ref), masked(column, flat(do_ref)))
 
 
 def finish_kernel(per_group, groups, ep_ref, own_ref, near_ref, far_ref, wr_ref, x0_ref, xs_ref, ms_ref, q_ref, gx_ref, gr_ref, wr_scr, acc):
@@ -527,27 +527,26 @@
         rows_at = lambda e, hot, ep_ref: (0, e, 0)
         fix = lambda shape: pl.BlockSpec(shape, lambda e, hot, ep_ref: (0,) * len(shape), pipeline_mode=pl.Buffered(1))
         n_row = (n_dev - 2) * SLOTS
-        *gx_part, q_loc, act, dz, act_more, dz_more = pl.pallas_call(
+        *gx_part, q_loc, grad_down, dz, dz_more = pl.pallas_call(
             functools.partial(pass1_kernel, n_loc, (2, 3, 0, 1)),
             out_shape=[sds((toks, dim), F32)] * ep
             + [
                 sds((ep * n_loc, toks), F32),
-                sds((n_loc, n_row, ff), BF16),
+                sds((n_loc, ff, dim), F32),
                 sds((n_loc, n_row, 2 * ff), BF16),
-                sds((pairs, 2 * EXTRA, ff), BF16),
                 sds((pairs, 2 * EXTRA, 2 * ff), BF16),
             ],
             grid_spec=pltpu.PrefetchScalarGridSpec(
                 num_scalar_prefetch=2,
                 grid=(n_loc,),
                 in_specs=w_specs(im3)
-                + [pl.BlockSpec((pairs - 1, 2 * SLOTS, dim), rows_at)] * 2
-                + [pl.BlockSpec((1, 2 * SLOTS, dim), rows_at), pl.BlockSpec((1, 2 * SLOTS, 2 * ff), im3), fix((2 * n_loc, toks))]
+                + [pl.BlockSpec((pairs - 1, 2 * SLOTS, dim), rows_at), pl.BlockSpec((pairs, 2 * SLOTS, dim), rows_at)]
+                + [pl.BlockSpec((1, 2 * SLOTS, dim), rows_at), pl.BlockSpec((1, 2 * SLOTS, ff), im3), pl.BlockSpec((1, 2 * SLOTS, 2 * ff), im3), fix((2 * n_loc, toks))]
                 + [hbm] * 3
                 + [pl.BlockSpec((ep, 1, 1, PAD, toks), lambda e, hot, ep_ref: (0, 0, ep_ref[0], 0, 0))],
                 out_specs=[hbm] * ep
-                + [fix((ep * n_loc, toks)), pl.BlockSpec((1, n_row, ff), im3), pl.BlockSpec((1, n_row, 2 * ff), im3)]
-                + [fix((pairs, 2 * EXTRA, ff)), fix((pairs, 2 * EXTRA, 2 * ff))],
+                + [fix((ep * n_loc, toks)), pl.BlockSpec((1, ff, dim), im3), pl.BlockSpec((1, n_row, 2 * ff), im3)]
+                + [fix((pairs, 2 * EXTRA, 2 * ff))],
                 scratch_shapes=[
                     pltpu.VMEM((ep, n_loc * SPAN + TAIL, dim), BF16),
                     pltpu.VMEM((ep, toks, dim), F32),
@@ -561,7 +560,7 @@
             compiler_params=params,
             cost_estimate=pl.CostEstimate(flops=4 * 10**10, bytes_accessed=10**8, transcendentals=0),
             name="pass1",
-        )(hot, ep_arr, w_gate, w_up, w_down, x_rows, d_rows, g_rows, dz01, q01, x_more, d_more, g_more, ms)
+        )(hot, ep_arr, w_gate, w_up, w_down, x_rows, d_rows, g_rows, act01, dz01, q01, x_more, d_more, g_more, ms)
 
         for_peer, q_all = pl.pallas_call(
             back_kernel,
@@ -588,29 +587,26 @@
         im3 = lambda e, hot: (e, 0, 0)
         rows_at = lambda e, hot: (0, e, 0)
         fix = lambda shape: pl.BlockSpec(shape, lambda e, hot: (0,) * len(shape), pipeline_mode=pl.Buffered(1))
-        grad_gate, grad_up, grad_down = pl.pallas_call(
+        grad_gate, grad_up = pl.pallas_call(
             pass2_kernel,
-            out_shape=[sds((n_loc, dim, ff), F32), sds((n_loc, dim, ff), F32), sds((n_loc, ff, dim), F32)],
+            out_shape=[sds((n_loc, dim, ff), F32)] * 2,
             grid_spec=pltpu.PrefetchScalarGridSpec(
                 num_scalar_prefetch=1,
                 grid=(n_loc,),
-                in_specs=[pl.BlockSpec((1, n_row, ff), im3), pl.BlockSpec((1, n_row, 2 * ff), im3)]
-                + [pl.BlockSpec((1, 2 * SLOTS, ff), im3), pl.BlockSpec((1, 2 * SLOTS, 2 * ff), im3)]
-                + [pl.BlockSpec((pairs, 2 * SLOTS, dim), rows_at)] * 2
-                + [hbm] * 4,
-                out_specs=w_specs(im3),
+                in_specs=[pl.BlockSpec((1, n_row, 2 * ff), im3), pl.BlockSpec((1, 2 * SLOTS, 2 * ff), im3)]
+                + [pl.BlockSpec((pairs, 2 * SLOTS, dim), rows_at)]
+                + [hbm] * 2,
+                out_specs=[pl.BlockSpec((1, dim, ff), im3)] * 2,
                 scratch_shapes=[
                     pltpu.VMEM((pairs, 2 * EXTRA, dim), BF16),
-                    pltpu.VMEM((pairs, 2 * EXTRA, dim), BF16),
-                    pltpu.VMEM((pairs, 2 * EXTRA, ff), BF16),
                     pltpu.VMEM((pairs, 2 * EXTRA, 2 * ff), BF16),
-                    pltpu.SemaphoreType.DMA((4,)),
+                    pltpu.SemaphoreType.DMA((2,)),
                 ],
             ),
             compiler_params=params,
             cost_estimate=pl.CostEstimate(flops=6 * 10**10, bytes_accessed=2 * 10**8, transcendentals=0),
             name="pass2",
-        )(hot, act, dz, act01, dz01, x_rows, d_rows, x_more, d_more, act_more, dz_more)
+        )(hot, dz, dz01, x_rows, x_more, dz_more)
 
         fixed = lambda shape: pl.BlockSpec(shape, lambda i, ep_ref: (0,) * len(shape))
         grad_x, grad_rt = pl.pallas_call(

time: 193 us -> 186 us (0.964); the launches traced: 190 us -> 186 us
  Pallas kernels: 188 us -> 181 us
  waiting for transfers between devices: 0.01 us -> 2.7 us
    pallas_call x1, Pallas kernels: 50.2 us -> 33.2 us  [device_step(): pl.pallas_call(pass2_kernel, out_shape=[sds((n_loc, dim, ff), F32)] * 2,...]
    pallas_call x1, Pallas kernels: 46.2 us -> 54.9 us  [device_step(): pl.pallas_call(functools.partial(pass1_kernel, n_loc, (2, 3, 0, 1)), out_...]
    ppermute x2, waiting for transfers between devices: 0.01 us -> 2.7 us  [swap(): return lax.ppermute(v, ('dp', 'ep'), [(s, s ^ bit) for s in range(n_dev)])]
  transfers between devices with their start and end apart: 2 -> 2, of which waited for: 0 -> 1; matrix products, arithmetic and copies ran while one was open for 0% -> 0% of each run, Pallas kernels for 26% -> 18%
where the time goes in v5:
time: 186 us
  Pallas kernels  181 us (97%)
  waiting for transfers between devices  2.7 us (1%)
    pallas_call x1, Pallas kernels, device_step(): pl.pallas_call(functools.partial(near_kernel, n_loc), out_shape=[sds((pai...  68.5 us
    pallas_call x1, Pallas kernels, device_step(): pl.pallas_call(functools.partial(pass1_kernel, n_loc, (2, 3, 0, 1)), out_...  54.9 us
    pallas_call x1, Pallas kernels, device_step(): pl.pallas_call(pass2_kernel, out_shape=[sds((n_loc, dim, ff), F32)] * 2,...  33.2 us
    pallas_call x1, Pallas kernels, device_step(): pl.pallas_call(back_kernel, out_shape=[sds((toks, dim), F32), sds((n_dev,...  17.7 us
    pallas_call x1, Pallas kernels, device_step(): pl.pallas_call(functools.partial(finish_kernel, n_loc, ep), out_shape=[sd...  6.87 us
  transfers between devices with their start and end apart: 2, of which 1 were waited for; matrix products, arithmetic and copies ran while one was open for 0% of the time, Pallas kernels for 18%

profile of v5, /device:TPU:0, one launch (start us, length us, event | category | flops | bytes accessed | tf_op | source)
XLA Modules:
  0.0 185.6 jit_solution(14905483942874301419)
XLA Ops:
  0.6 68.5 %near.1 = (bf16[4,1120,1536]{2,1,0:T(8,128)(2,1)}, bf16[4,208,1536]{2,1,0:T(8,128)(2,1)}, bf16[4,1120,1536]{2,1,0:T(8,128)(2,1)}, bf16[4,208,1536]{2,1,0:T(8,128...) custom-call(bf16[256,1536]{1,0:T(8,128)(2,1)} %x0_ref.1, ...), custom_call_target="tpu_custom_call" | custom-call | flops 20000000000 | bytes 50000000 | tf_op jit(solution)/shard_map/near/pallas_call | solution.py:484
  69.2 54.9 %pass1.1 = (f32[256,1536]{1,0:T(8,128)}, f32[256,1536]{1,0:T(8,128)}, f32[256,1536]{1,0:T(8,128)}, f32[256,1536]{1,0:T(8,128)}, f32[40,256]{1,0:T(8,128)}, /*ind...) custom-call(s32[8,128]{1,0:T(8,128)} %get-tuple-element.33.hot_ref, ...), custom_call_target="tpu_custom_call" | custom-call | flops 40000000000 | bytes 100000000 | tf_op jit(solution)/shard_map/pass1/pallas_call | solution.py:530
  124.1 17.7 %back.1 = (f32[256,1536]{1,0:T(8,128)}, f32[8,40,256]{2,1,0:T(8,128)}) custom-call(f32[40,256]{1,0:T(8,128)} %get-tuple-element.45.q_ref, f32[256,1536]{1,0:T(8,128)} %get-tuple-element.46.keep_ref, f32[256,1536]{1,0:T(8,128)} %get-tuple-element.47.give_ref), custom_call_target="tpu_custom_call" | custom-call | flops 8000000000 | bytes 50000000 | tf_op jit(solution)/shard_map/back/pallas_call | solution.py:565
  141.9 0.4 collective-permute-start
  142.2 0.6 collective-permute-start.1
  142.8 33.2 %pass2.1 = (f32[10,1536,512]{2,1,0:T(8,128)}, f32[10,1536,512]{2,1,0:T(8,128)}) custom-call(s32[8,128]{1,0:T(8,128)} %get-tuple-element.33.hot_ref, bf16[10,336,1024]{2,1,0:T(8,128)(2,1)} %get-tuple-element.55.dz_ref, bf16[10,112,1024]{2,1,0:T(8,128)(2,1)} %get-tuple-element.38.dz01_ref, bf16[4,1120,1536]{2,1,0:T(8,128)(2,1)} %get-tuple-element.34.x_ref, ...), custom_call_target="tpu_custom_call" | custom-call | flops 60000002048 | bytes 200000000 | tf_op jit(solution)/shard_map/pass2/pallas_call | solution.py:590
  176.0 0.0 collective-permute-done.near_ref
  176.0 2.7 %collective-permute-done.1.far_ref = f32[256,1536]{1,0:T(8,128)} collective-permute-done((f32[256,1536]{1,0:T(8,128)}, f32[256,1536]{1,0:T(8,128)}, u32[]{:S(2)}, u32[]{:S(2)}) %collective-permute-start.1) | collective-permute-done | bytes 1572896 | tf_op jit(solution)/shard_map/ppermute | solution.py:466
  178.7 6.9 %finish.1 = (bf16[256,1536]{1,0:T(8,128)(2,1)}, f32[40,1536]{1,0:T(8,128)}) custom-call(s32[1]{0:T(128)} %bitcast.ep_ref, f32[256,1536]{1,0:T(8,128)} %get-tuple-element.44.own_ref, f32[256,1536]{1,0:T(8,128)} %collective-permute-done.near_ref, f32[256,1536]{1,0:T(8,128)} %collective-permute-done.1.far_ref, bf16[40,1536]{1,0:T(8,128)(2,1)} %bitcast.5, ...), custom_call_target="tpu_custom_call" | custom-call | flops 4000000000 | bytes 10000000 | tf_op jit(solution)/shard_map/finish/pallas_call | solution.py:612
Async XLA Ops:
  141.9 34.1 %collective-permute-start = (f32[256,1536]{1,0:T(8,128)}, f32[256,1536]{1,0:T(8,128)}, u32[]{:S(2)}, u32[]{:S(2)}) collective-permute-start(f32[256,1536]{1,0:T(8,128)} %get-tuple-element.50), channel_id=1, source_target_pairs={{0,1},{1,0},{2,3},{3,2},{4,5},{5,4},{6,7},{7,6}} | collective-permute-start | bytes 4718600 | tf_op jit(solution)/shard_map/ppermute | solution.py:466
  142.2 36.5 %collective-permute-start.1 = (f32[256,1536]{1,0:T(8,128)}, f32[256,1536]{1,0:T(8,128)}, u32[]{:S(2)}, u32[]{:S(2)}) collective-permute-start(f32[256,1536]{1,0:T(8,128)} %get-tuple-element.51), channel_id=1, source_target_pairs={{0,2},{1,3},{2,0},{3,1},{4,6},{5,7},{6,4},{7,5}} | collective-permute-start | bytes 4718600 | tf_op jit(solution)/shard_map/ppermute | solution.py:466

commit v6 on v5

--- a/solution.py
+++ b/solution.py
@@ -64,7 +64,7 @@
         out_ref[1, a, per_group:, :] = jnp.zeros((PAD - per_group, toks), F32)
 
 
-def gather_rows(me, per_group, m_refs, x_refs, g_refs, x_out, d_out, g_out):
+def gather_rows(send, me, per_group, m_refs, x_refs, g_refs, x_out, d_out, g_out):
     step = per_group // 2
 
     def emit(masks, probs, size, first):
@@ -86,6 +86,7 @@
         masks = [[slot_mask(m[0, me, pl.ds(i * step + k, 1), :], SLOTS, 0) for k in range(step)] for m in m_refs]
         probs = [[m[1, me, pl.ds(i * step + k, 1), :] for k in range(step)] for m in m_refs]
         emit(masks, probs, SLOTS, i * (step * 2 * SLOTS))
+        send(pl.ds(pl.multiple_of(i * (step * 2 * SLOTS), 16), step * 2 * SLOTS))
         return carry
 
     lax.fori_loop(0, 2, part, 0)
@@ -106,13 +107,19 @@
         slot, self.turn = self.turn, 1 - self.turn
         self.drain(slot)
         views = [self.bufs[k].at[slot] for k in range(kinds)]
-        gather_rows(*args, *(views + [None])[:3])
-        copies = []
-        for k in range(kinds):
-            copies.append(pltpu.make_async_copy(views[k].at[pl.ds(0, self.main)], self.outs[2 * k].at[index[k]], self.sems.at[slot, 2 * k]))
-            copies.append(pltpu.make_async_copy(views[k].at[pl.ds(self.main, 2 * EXTRA)], self.outs[2 * k + 1].at[index[k]], self.sems.at[slot, 2 * k + 1]))
-        for c in copies:
+
+        def main_copies(rows):
+            return [pltpu.make_async_copy(views[k].at[rows], self.outs[2 * k].at[index[k], rows], self.sems.at[slot, 2 * k]) for k in range(kinds)]
+
+        def send(rows):
+            for c in main_copies(rows):
+                c.start()
+
+        gather_rows(send, *args, *(views + [None])[:3])
+        extra = [pltpu.make_async_copy(views[k].at[pl.ds(self.main, 2 * EXTRA)], self.outs[2 * k + 1].at[index[k]], self.sems.at[slot, 2 * k + 1]) for k in range(kinds)]
+        for c in extra:
             c.start()
+        copies = main_copies(pl.ds(0, self.main)) + extra
         self.busy[slot] = copies
 
     def drain(self, slot):

time: 186 us -> 184 us (0.989)
  waiting for transfers between devices: 2.7 us -> 0.01 us
    pallas_call x1, Pallas kernels: 54.9 us -> 63.5 us  [device_step(): pl.pallas_call(functools.partial(pass1_kernel, n_loc, (2, 3, 0, 1)), out_...]
    pallas_call x1, Pallas kernels: 17.7 us -> 9.36 us  [device_step(): pl.pallas_call(back_kernel, out_shape=[sds((toks, dim), F32), sds((n_dev,...]
    pallas_call x1, Pallas kernels: 33.2 us -> 36.7 us  [device_step(): pl.pallas_call(pass2_kernel, out_shape=[sds((n_loc, dim, ff), F32)] * 2,...]
    pallas_call x1, Pallas kernels: 68.5 us -> 65.3 us  [device_step(): pl.pallas_call(functools.partial(near_kernel, n_loc), out_shape=[sds((pai...]
    ppermute x2, waiting for transfers between devices: 2.7 us -> 0.01 us  [swap(): return lax.ppermute(v, ('dp', 'ep'), [(s, s ^ bit) for s in range(n_dev)])]
  transfers between devices with their start and end apart: 2 -> 2, of which waited for: 1 -> 0; matrix products, arithmetic and copies ran while one was open for 0% -> 0% of each run, Pallas kernels for 18% -> 20%
where the time goes in v6:
time: 184 us; the launch traced here: 183 us
  Pallas kernels  182 us (99%)
    pallas_call x1, Pallas kernels, device_step(): pl.pallas_call(functools.partial(near_kernel, n_loc), out_shape=[sds((pai...  65.3 us
    pallas_call x1, Pallas kernels, device_step(): pl.pallas_call(functools.partial(pass1_kernel, n_loc, (2, 3, 0, 1)), out_...  63.5 us
    pallas_call x1, Pallas kernels, device_step(): pl.pallas_call(pass2_kernel, out_shape=[sds((n_loc, dim, ff), F32)] * 2,...  36.7 us
    pallas_call x1, Pallas kernels, device_step(): pl.pallas_call(back_kernel, out_shape=[sds((toks, dim), F32), sds((n_dev,...  9.36 us
    pallas_call x1, Pallas kernels, device_step(): pl.pallas_call(functools.partial(finish_kernel, n_loc, ep), out_shape=[sd...  6.87 us
  transfers between devices with their start and end apart: 2, of which 0 were waited for; matrix products, arithmetic and copies ran while one was open for 0% of the time, Pallas kernels for 20%

profile of v6, /device:TPU:0, one launch (start us, length us, event | category | flops | bytes accessed | tf_op | source)
XLA Modules:
  0.0 183.4 jit_solution(1580468646732407446)
XLA Ops:
  0.6 65.3 %near.1 = (bf16[4,1120,1536]{2,1,0:T(8,128)(2,1)}, bf16[4,208,1536]{2,1,0:T(8,128)(2,1)}, bf16[4,1120,1536]{2,1,0:T(8,128)(2,1)}, bf16[4,208,1536]{2,1,0:T(8,128...) custom-call(bf16[256,1536]{1,0:T(8,128)(2,1)} %x0_ref.1, ...), custom_call_target="tpu_custom_call" | custom-call | flops 20000000000 | bytes 50000000 | tf_op jit(solution)/shard_map/near/pallas_call | solution.py:491
  66.0 63.5 %pass1.1 = (f32[256,1536]{1,0:T(8,128)}, f32[256,1536]{1,0:T(8,128)}, f32[256,1536]{1,0:T(8,128)}, f32[256,1536]{1,0:T(8,128)}, f32[40,256]{1,0:T(8,128)}, /*ind...) custom-call(s32[8,128]{1,0:T(8,128)} %get-tuple-element.33.hot_ref, ...), custom_call_target="tpu_custom_call" | custom-call | flops 40000000000 | bytes 100000000 | tf_op jit(solution)/shard_map/pass1/pallas_call | solution.py:537
  129.5 9.4 %back.1 = (f32[256,1536]{1,0:T(8,128)}, f32[8,40,256]{2,1,0:T(8,128)}) custom-call(f32[40,256]{1,0:T(8,128)} %get-tuple-element.45.q_ref, f32[256,1536]{1,0:T(8,128)} %get-tuple-element.46.keep_ref, f32[256,1536]{1,0:T(8,128)} %get-tuple-element.47.give_ref), custom_call_target="tpu_custom_call" | custom-call | flops 8000000000 | bytes 50000000 | tf_op jit(solution)/shard_map/back/pallas_call | solution.py:572
  138.8 0.4 collective-permute-start
  139.2 0.6 collective-permute-start.1
  139.8 36.7 %pass2.1 = (f32[10,1536,512]{2,1,0:T(8,128)}, f32[10,1536,512]{2,1,0:T(8,128)}) custom-call(s32[8,128]{1,0:T(8,128)} %get-tuple-element.33.hot_ref, bf16[10,336,1024]{2,1,0:T(8,128)(2,1)} %get-tuple-element.55.dz_ref, bf16[10,112,1024]{2,1,0:T(8,128)(2,1)} %get-tuple-element.38.dz01_ref, bf16[4,1120,1536]{2,1,0:T(8,128)(2,1)} %get-tuple-element.34.x_ref, ...), custom_call_target="tpu_custom_call" | custom-call | flops 60000002048 | bytes 200000000 | tf_op jit(solution)/shard_map/pass2/pallas_call | solution.py:597
  176.5 0.0 collective-permute-done.near_ref
  176.5 0.0 collective-permute-done.1.far_ref
  176.5 6.9 %finish.1 = (bf16[256,1536]{1,0:T(8,128)(2,1)}, f32[40,1536]{1,0:T(8,128)}) custom-call(s32[1]{0:T(128)} %bitcast.ep_ref, f32[256,1536]{1,0:T(8,128)} %get-tuple-element.44.own_ref, f32[256,1536]{1,0:T(8,128)} %collective-permute-done.near_ref, f32[256,1536]{1,0:T(8,128)} %collective-permute-done.1.far_ref, bf16[40,1536]{1,0:T(8,128)(2,1)} %bitcast.5, ...), custom_call_target="tpu_custom_call" | custom-call | flops 4000000000 | bytes 10000000 | tf_op jit(solution)/shard_map/finish/pallas_call | solution.py:619
Async XLA Ops:
  138.8 37.7 %collective-permute-start = (f32[256,1536]{1,0:T(8,128)}, f32[256,1536]{1,0:T(8,128)}, u32[]{:S(2)}, u32[]{:S(2)}) collective-permute-start(f32[256,1536]{1,0:T(8,128)} %get-tuple-element.50), channel_id=1, source_target_pairs={{0,1},{1,0},{2,3},{3,2},{4,5},{5,4},{6,7},{7,6}} | collective-permute-start | bytes 4718600 | tf_op jit(solution)/shard_map/ppermute | solution.py:473
  139.2 37.3 %collective-permute-start.1 = (f32[256,1536]{1,0:T(8,128)}, f32[256,1536]{1,0:T(8,128)}, u32[]{:S(2)}, u32[]{:S(2)}) collective-permute-start(f32[256,1536]{1,0:T(8,128)} %get-tuple-element.51), channel_id=1, source_target_pairs={{0,2},{1,3},{2,0},{3,1},{4,6},{5,7},{6,4},{7,5}} | collective-permute-start | bytes 4718600 | tf_op jit(solution)/shard_map/ppermute | solution.py:473
